TPU v7x, 512 devices: a 8x2x16 block of a 8x8x16 slice. The times are simulated.
512 devices in a mesh: groups: 2 (over y), ctx: 32 (over z, core), tp: 8 (over x).
Axes of the slice: x: 8, y: 2, z: 16, core: 2. Of those that a mesh axis runs over, the one named last changes fastest.
The devices are a block of a 8x8x16 slice.
Arguments:
- query_matrix: bfloat16 [8192, 8192], P(('groups', 'ctx'), 'tp'), parts along dimension 0, may hold values from -20 to 20
- key_matrix: bfloat16 [8192, 1024], P(('groups', 'ctx'), 'tp'), parts along dimension 0, may hold values from -20 to 20
- value_matrix: bfloat16 [8192, 1024], P(('groups', 'ctx'), 'tp'), parts along dimension 0, may hold values from -6 to 6
- doc_ids: int32 [8192], P('groups'), parts along dimension 0, may hold values from 0 to 5, never falling along the last dimension, each value on 1 to 2048 neighbouring positions
- out_weight: bfloat16 [8192, 4096], P('tp', 'ctx'), may hold values from -0.0625 to 0.0625
Outputs:
- projected: bfloat16 [8192, 4096], P(('groups', 'ctx'), 'tp'), parts along dimension 0
There are 2 independent parts, one for each index of `groups`. A program takes and returns all parts, laid end to end along the dimension named above; an argument that names none is the same for every part. Nothing has to cross between parts.
Inputs may be any that keep to these rules, and one draw needn't show every extreme that they name: `doc_ids`: non-decreasing along the sequence; each document holds 1 to 2048 tokens, one exactly 2048.
All inputs are finite; a program needn't handle non-finite values.
Results may differ from a plain program's by a relative error of at most 0.015.
Values may be sent and summed in bfloat16 or wider, within the bound.
No kernel may reach another device: no remote copies, remote signals or barrier semaphores. Data moves between devices by JAX's collectives and lax.ppermute only.
A program may use at most 64 MiB of HBM per device.

v0:
```python
import math

import jax
import jax.numpy as jnp
from jax import lax
from jax.sharding import PartitionSpec as P

HEAD_SIZE = 128


rope_base = 1000000.0


def in_one_piece(arrays, axis, dim, along):
    ends, at = ([], 0)
    for a in arrays[:-1]:
        at += a.shape[along]
        ends.append(at)
    both = jnp.concatenate(arrays, axis=along)
    return tuple(jnp.split(lax.all_gather(both, axis, axis=dim, tiled=True), ends, axis=along))


def split_up(x, dim, size):
    lengths = x.shape
    pieces = x.reshape(*lengths[:dim], size, lengths[dim] // size, *lengths[dim + 1 :])
    return jnp.moveaxis(pieces, dim, 0)


def sent_and_summed(x, axis, dim):
    pieces = split_up(x, dim, lax.axis_size(axis))
    arrived = lax.all_to_all(pieces, axis, split_axis=0, concat_axis=0, tiled=True)
    return arrived.astype(jnp.float32).sum(axis=0)


def rotary_tables(rows, token_positions, heads):
    half_dim = HEAD_SIZE // 2
    frequency = jnp.power(
        jnp.float32(rope_base), -jnp.arange(half_dim, dtype=jnp.float32) * (2.0 / HEAD_SIZE)
    )
    angles = token_positions.astype(jnp.float32)[:, None] * frequency[None, :]
    cosine = jnp.cos(angles)[:, None, :]
    sine = jnp.sin(angles)[:, None, :]
    values = rows.astype(jnp.float32).reshape(rows.shape[0], heads, HEAD_SIZE)
    first = values[..., :half_dim]
    second = values[..., half_dim:]
    turned = jnp.concatenate([first * cosine - second * sine, second * cosine + first * sine], -1)
    return turned.reshape(rows.shape[0], heads * HEAD_SIZE).astype(jnp.bfloat16)


def keep_state(held_state, unused_block):
    return held_state


def on_device(query_matrix, key_matrix, value_matrix, doc_ids, out_weight):
    ctx_index = lax.axis_index("ctx")
    tok_rows = query_matrix.shape[0]
    query_heads = query_matrix.shape[1] // HEAD_SIZE
    key_heads = key_matrix.shape[1] // HEAD_SIZE
    group_width = query_heads // key_heads
    inverse_root = HEAD_SIZE ** (-0.5)
    local_rows = jnp.arange(tok_rows, dtype=jnp.int32)
    given_pos = ctx_index * tok_rows + local_rows
    query_matrix_rot = rotary_tables(query_matrix, given_pos, query_heads)
    keys_here = rotary_tables(key_matrix, given_pos, key_heads)
    query_doc = jnp.take(doc_ids, given_pos, axis=0)
    query_four = query_matrix_rot.reshape(tok_rows, key_heads, group_width, HEAD_SIZE)
    first_doc = jnp.min(query_doc)
    last_doc = jnp.max(query_doc)
    last_pos = jnp.max(given_pos)

    def attend(state, block):
        key_block, value_block, doc_block, pos_block = block
        row_max, totals, accum = state
        scores = (
            jnp.einsum("qkgd,skd->kgqs", query_four, key_block, preferred_element_type=jnp.float32)
            * inverse_root
        )
        allowed = (
            (query_doc[:, None] == doc_block[None, :]) & (pos_block[None, :] <= given_pos[:, None])
        )[None, None]
        new_max = jnp.maximum(row_max, jnp.max(jnp.where(allowed, scores, -1e30), -1))
        weights = jnp.where(allowed, jnp.exp(scores - new_max[..., None]), 0.0)
        factor = jnp.exp(row_max - new_max)
        totals = totals * factor + jnp.sum(weights, -1)
        accum = accum * jnp.transpose(factor, (2, 0, 1))[..., None] + jnp.einsum(
            "kgqs,skd->qkgd",
            weights.astype(jnp.bfloat16),
            value_block,
            preferred_element_type=jnp.float32,
        )
        return (new_max, totals, accum)

    start_state = (
        jnp.full((key_heads, group_width, tok_rows), -1e30, jnp.float32),
        jnp.zeros((key_heads, group_width, tok_rows), jnp.float32),
        jnp.zeros((tok_rows, key_heads, group_width, HEAD_SIZE), jnp.float32),
    )
    key_piece, value_piece = in_one_piece((keys_here, value_matrix), "ctx", 0, 1)
    count = key_piece.shape[0]
    block_rows = math.gcd(count, 512)
    block_count = count // block_rows
    positions = jnp.arange(count, dtype=jnp.int32)
    blocks = (
        key_piece.reshape(block_count, block_rows, key_heads, HEAD_SIZE),
        value_piece.reshape(block_count, block_rows, key_heads, HEAD_SIZE),
        jnp.take(doc_ids, positions, axis=0).reshape(block_count, block_rows),
        positions.reshape(block_count, block_rows),
    )

    def step_block(inner_state, block):
        live = (
            (jnp.min(block[3]) <= last_pos)
            & (jnp.min(block[2]) <= last_doc)
            & (jnp.max(block[2]) >= first_doc)
        )
        return (lax.cond(live, attend, keep_state, inner_state, block), None)

    final_state, unused_out = lax.scan(step_block, start_state, blocks)
    row_max, totals, accum = final_state
    attention = (
        (accum / jnp.transpose(totals, (2, 0, 1))[..., None])
        .reshape(tok_rows, query_heads * HEAD_SIZE)
        .astype(jnp.bfloat16)
    )
    terms = jnp.dot(
        attention,
        lax.all_gather(out_weight, "ctx", axis=1, tiled=True),
        preferred_element_type=jnp.float32,
    )
    return sent_and_summed(terms.astype(jnp.bfloat16), "tp", 1).astype(jnp.bfloat16)


def solution(mesh):
    in_specs = (
        P(("groups", "ctx"), "tp"),
        P(("groups", "ctx"), "tp"),
        P(("groups", "ctx"), "tp"),
        P("groups"),
        P("tp", "ctx"),
    )
    out_specs = P(("groups", "ctx"), "tp")
    return jax.shard_map(
        on_device, mesh=mesh, in_specs=in_specs, out_specs=out_specs, check_vma=False
    )
```

profile of v0, /device:TPU:65, one launch (start us, length us, event | category | flops | bytes accessed | tf_op | source)
XLA Modules:
  0.0 262.6 jit_solution(11426903617318993670)
XLA Ops:
  6.5 0.0 copy-start
  6.6 0.0 all-gather.3.cloned.1.call-start
  6.6 0.6 fusion.36
  7.2 0.9 copy.19
  8.1 0.9 copy.20
  8.9 0.2 fusion.32
  9.2 0.6 pad_maximum_fusion.1
  9.8 0.1 all-gather.3.cloned.1.call-update
  9.9 0.1 all-gather.5.cloned.1.call-start
  9.9 0.7 all-gather.5.cloned.1.call-update
  10.7 1.1 copy.21
  11.8 0.2 multiply_cosine_fusion
  12.0 0.1 fusion.25
  12.1 0.2 copy.24
  12.4 0.0 copy-done
  12.4 1.1 gather_fusion.1
  13.5 23.0 %gather_fusion = s32[4096]{0:T(1024)S(1)} fusion(s32[4096]{0:T(1024)S(1)} %copy-done, s32[4096]{0:T(1024)S(1)} %iota_clamp_fusion), kind=kCustom, calls=%fused_computation | custom fusion | bytes 49152 | tf_op jit(solution)/shard_map/jit(_take)/gather | solution.py:106
  36.6 0.7 fusion.39
  37.3 82.9 %all-gather.3.cloned.1.call-done = bf16[4096,256]{0,1:T(8,128)(2,1)} async-done(((bf16[128,256]{0,1:T(8,128)(2,1)}), bf16[4096,256]{0,1:T(8,128)(2,1)}) %all-gather.3.cloned.1.call-update) | async-done | bytes 2097168 | tf_op jit(solution)/shard_map/all_gather | solution.py:20
  120.2 1.7 fusion.41
  121.9 0.7 copy.22
  122.6 0.5 copy.25
  123.1 0.7 copy.28
  123.8 37.2 %while.15 = (s32[]{:T(128)}, f32[1,8,128]{2,1,0:T(8,128)S(1)}, f32[1,8,128]{2,1,0:T(8,128)S(1)}, f32[128,1,8,128]{0,3,2,1:T(8,128)S(1)}, s32[8,512]{1,0:T(8,128)...) while((s32[]{:T(128)}, f32[1,8,128]{2,1,0:T(8,128)S(1)}, ...), condition=%wide.region_11.12_spmd.clone, body=%wide.region_3.11_spmd.clone.sunk | while | flops 274666112 | bytes 8207207 | solution.py:118
  123.9 0.7 fusion.45
  128.2 1.8 conditional.3
  128.3 0.2 compare_and_fusion
  128.5 0.5 fusion.2
  129.0 0.4 fusion.6
  129.4 0.6 fusion.7
  130.1 0.7 fusion.45
  134.5 0.7 fusion.45
  138.9 0.7 fusion.45
  143.3 0.7 fusion.45
  147.8 0.7 fusion.45
  152.2 0.7 fusion.45
  156.6 0.7 fusion.45
  161.0 0.1 divide_convert_fusion
  161.1 54.5 %all-gather.5.cloned.1.call-done = bf16[1024,4096]{1,0:T(8,128)(2,1)} async-done(((bf16[1024,128]{1,0:T(8,128)(2,1)}), bf16[1024,4096]{1,0:T(8,128)(2,1)}) %all-gather.5.cloned.1.call-update) | async-done | bytes 8388624 | tf_op jit(solution)/shard_map/all_gather | solution.py:127
  215.6 4.7 %convolution_convert_fusion = bf16[128,4096]{1,0:T(8,128)(2,1)S(1)} fusion(bf16[128,1024]{0,1:T(8,128)(2,1)S(1)} %bitcast.90, bf16[1024,4096]{1,0:T(8,128)(2,1)} %all-gather.5.cloned.1.call-done), kind=kOutput, calls=%fused_computation.35 | convolution fusion | flops 1074266112 | bytes 9699328 | tf_op jit(solution)/shard_map/dot_general | solution.py:125
  220.2 0.1 copy.31
  220.3 34.6 %all_to_all.5 = bf16[8,128,512]{2,1,0:T(8,128)(2,1)S(1)} all-to-all(bf16[8,128,512]{2,1,0:T(8,128)(2,1)S(1)} %bitcast.85), channel_id=1, replica_groups=mesh['groups'=2,'ctx'=32,'tp'=8] {'tp'}, dimensions={0} | all-to-all | bytes 2097152 | tf_op jit(solution)/shard_map/all_to_all | solution.py:31
  254.9 0.8 reduce_sum.23
  (32 shorter events, 0.3 us)
Async XLA Ops:
  6.5 5.8 %copy-start = (s32[4096]{0:T(1024)S(1)}, s32[4096]{0:T(1024)}, u32[]{:S(2)}) copy-start(s32[4096]{0:T(1024)} %param.12) | copy-start | bytes 49156
  6.6 113.7 %all-gather.3.cloned.1.call-start = ((), (), s32[]{:S(2)}) async-start(), calls=%async_computation.1 | async-start | bytes 2162688 | tf_op jit(solution)/shard_map/all_gather | solution.py:20
  9.9 205.7 %all-gather.5.cloned.1.call-start = ((), (), s32[]{:S(2)}) async-start(), calls=%async_computation.2 | async-start | bytes 8650752 | tf_op jit(solution)/shard_map/all_gather | solution.py:127
Sparse Core Ops, SparseCore 0:
  10.0 110.2 all-gather.2
  122.3 93.2 all-gather.4
where the time goes:
time: 263 us
  waiting for transfers between devices  138 us (52%)
  blocking collectives  34.6 us (13%)
  local copies, waits for them, and re-layouts  30.9 us (12%)
  loops' own time  29.9 us (11%)
  between operations  13.6 us (5%)
  other arithmetic  9.57 us (4%)
  matrix products  5.76 us (2%)
    all_gather x1, waiting for transfers between devices, in_one_piece(): lax.all_gather(both, axis, axis=dim, tiled=True)  82.9 us
    all_gather x1, waiting for transfers between devices, on_device(): lax.all_gather(out_weight, 'ctx', axis=1, tiled=True)  54.5 us
    all_to_all x1, blocking collectives, sent_and_summed(): lax.all_to_all(pieces, axis, split_axis=0, concat_axis=0, tiled=True)  34.6 us
    another operation x1, loops' own time, on_device(): final_state, unused_out = lax.scan(step_block, start_state, blocks)  29.7 us
    gather x2, local copies, waits for them, and re-layouts, on_device(): jnp.take(doc_ids, positions, axis=0).reshape(block_count, block_rows)  23 us
    reduce_max x8, other arithmetic, step_block(): jnp.max(block[2]) >= first_doc  5.52 us
  transfers between devices with their start and end apart: 2, of which 2 were waited for; matrix products, arithmetic and copies ran while one was open for 14% of the time, Pallas kernels for 0%

commit v1 on v0

v1 whole, which is shorter than its diff:
```python
import functools
import math

import jax
import jax.numpy as jnp
from jax import lax
from jax.experimental import pallas as pl
from jax.experimental.pallas import tpu as pltpu
from jax.sharding import Mesh
from jax.sharding import PartitionSpec as P

HEAD_SIZE = 128
CORES = 2


rope_base = 1000000.0


def rotary_tables(token_positions):
    half_dim = HEAD_SIZE // 2
    frequency = jnp.power(
        jnp.float32(rope_base), -jnp.arange(half_dim, dtype=jnp.float32) * (2.0 / HEAD_SIZE)
    )
    angles = token_positions.astype(jnp.float32)[:, None] * frequency[None, :]
    return jnp.cos(angles), jnp.sin(angles)


def rotate(rows, tables, heads):
    half_dim = HEAD_SIZE // 2
    cosine, sine = (t[:, None, :] for t in tables)
    values = rows.astype(jnp.float32).reshape(rows.shape[0], heads, HEAD_SIZE)
    first = values[..., :half_dim]
    second = values[..., half_dim:]
    turned = jnp.concatenate([first * cosine - second * sine, second * cosine + first * sine], -1)
    return turned.reshape(rows.shape[0], heads * HEAD_SIZE).astype(jnp.bfloat16)


def attend(heads, info, start_ref, q_ref, ka_ref, kb_ref, va_ref, vb_ref, out_ref, m_ref, l_ref, acc_ref):
    rows = q_ref.shape[0]
    first_pair, ctx = info[0], info[1]
    core = lax.rem(ctx, CORES)
    scale = HEAD_SIZE**-0.5 * math.log2(math.e)
    m_ref[...] = jnp.full(m_ref.shape, -1e30, jnp.float32)
    l_ref[...] = jnp.zeros(l_ref.shape, jnp.float32)
    acc_ref[...] = jnp.zeros(acc_ref.shape, jnp.float32)
    width = CORES * rows
    lane = lax.broadcasted_iota(jnp.int32, (rows, width), 1)
    given = ctx * rows + lax.broadcasted_iota(jnp.int32, (rows, width), 0)
    mine = lane < rows
    first = start_ref[...]

    def one_pair(step, carry):
        pair = lax.div(ctx, CORES) - step
        own = (pair * CORES + core) * rows
        other = (pair * CORES + (1 - core)) * rows - rows
        position = lane + jnp.where(mine, own, other)
        allowed = (position >= first) & (position <= given)
        keys = jnp.concatenate([ka_ref[pair], kb_ref[pair]], 0)
        values = jnp.concatenate([va_ref[pair], vb_ref[pair]], 0)
        for h in range(heads):
            q = q_ref[:, h * HEAD_SIZE : (h + 1) * HEAD_SIZE]
            scores = lax.dot_general(
                q, keys, (((1,), (1,)), ((), ())), preferred_element_type=jnp.float32
            )
            scores = jnp.where(allowed, scores, -1e30)
            old = m_ref[h]
            new = jnp.maximum(old, jnp.max(scores, 1, keepdims=True))
            weights = jnp.exp2((scores - new) * scale)
            factor = jnp.exp2((old - new) * scale)
            m_ref[h] = new
            l_ref[h] = l_ref[h] * factor + jnp.sum(weights, 1, keepdims=True)
            acc_ref[h] = acc_ref[h] * factor + jnp.dot(
                weights.astype(jnp.bfloat16), values, preferred_element_type=jnp.float32
            )
        return carry

    lax.fori_loop(0, lax.div(ctx, CORES) - first_pair + 1, one_pair, 0)
    for h in range(heads):
        out_ref[:, h * HEAD_SIZE : (h + 1) * HEAD_SIZE] = (acc_ref[h] / l_ref[h]).astype(
            jnp.bfloat16
        )


def project(count, a_ref, w_ref, out_ref):
    width = w_ref.shape[2]
    for i in range(count):
        out_ref[0, :, i * width : (i + 1) * width] = jnp.dot(
            a_ref[...], w_ref[i], preferred_element_type=jnp.float32
        ).astype(jnp.bfloat16)


def on_device(query_matrix, key_matrix, value_matrix, doc_ids, out_weight):
    tok_rows = query_matrix.shape[0]
    query_heads = query_matrix.shape[1] // HEAD_SIZE
    members = lax.axis_size("tp")
    ctx_index = lax.axis_index("z") * CORES + lax.axis_index("core")
    weight_blocks = lax.all_gather(out_weight, ("z", "core"), axis=0, tiled=False)
    given_pos = ctx_index * tok_rows + jnp.arange(tok_rows, dtype=jnp.int32)
    tables = rotary_tables(given_pos)
    keys_here = rotate(key_matrix, tables, 1)
    swap = [(i, CORES - 1 - i) for i in range(CORES)]
    keys_a = lax.all_gather(keys_here, "z", axis=0, tiled=False)
    keys_b = lax.ppermute(keys_a, "core", swap)
    values_a = lax.all_gather(value_matrix, "z", axis=0, tiled=False)
    values_b = lax.ppermute(values_a, "core", swap)
    queries = rotate(query_matrix, tables, query_heads)
    query_doc = lax.dynamic_slice_in_dim(doc_ids, ctx_index * tok_rows, tok_rows, 0)
    starts = jnp.sum((doc_ids[None, :] < query_doc[:, None]).astype(jnp.int32), 1)
    first_pair = jnp.min(starts) // (CORES * tok_rows)
    info = jnp.stack([first_pair, ctx_index]).astype(jnp.int32)
    vmem = pl.BlockSpec(memory_space=pltpu.VMEM)
    attention = pl.pallas_call(
        functools.partial(attend, query_heads),
        out_shape=jax.ShapeDtypeStruct((tok_rows, query_heads * HEAD_SIZE), jnp.bfloat16),
        in_specs=[pl.BlockSpec(memory_space=pltpu.SMEM)] + [vmem] * 6,
        out_specs=vmem,
        scratch_shapes=[
            pltpu.VMEM((query_heads, tok_rows, 1), jnp.float32),
            pltpu.VMEM((query_heads, tok_rows, 1), jnp.float32),
            pltpu.VMEM((query_heads, tok_rows, HEAD_SIZE), jnp.float32),
        ],
        cost_estimate=pl.CostEstimate(flops=2 * 10**9, bytes_accessed=3 * 10**6, transcendentals=10**6),
        name="attend",
    )(info, starts[:, None], queries, keys_a, keys_b, values_a, values_b)
    blocks, depth, width = weight_blocks.shape
    share = blocks // members
    terms = pl.pallas_call(
        functools.partial(project, share),
        grid=(members,),
        out_shape=jax.ShapeDtypeStruct((members, tok_rows, share * width), jnp.bfloat16),
        in_specs=[
            pl.BlockSpec((tok_rows, depth), lambda i: (0, 0)),
            pl.BlockSpec((share, depth, width), lambda i: (i, 0, 0)),
        ],
        out_specs=pl.BlockSpec((1, tok_rows, share * width), lambda i: (i, 0, 0)),
        cost_estimate=pl.CostEstimate(flops=10**9, bytes_accessed=10**7, transcendentals=0),
        name="project",
    )(attention, weight_blocks)
    arrived = lax.all_to_all(terms, "tp", split_axis=0, concat_axis=0, tiled=True)
    return arrived.astype(jnp.float32).sum(axis=0).astype(jnp.bfloat16)


def solution(mesh):
    groups, ctx, tp = mesh.devices.shape
    fine = Mesh(mesh.devices.reshape(groups, ctx // CORES, CORES, tp), ("groups", "z", "core", "tp"))
    tokens = ("groups", "z", "core")
    in_specs = (P(tokens, "tp"), P(tokens, "tp"), P(tokens, "tp"), P("groups"), P("tp", ("z", "core")))
    return jax.shard_map(
        on_device, mesh=fine, in_specs=in_specs, out_specs=P(tokens, "tp"), check_vma=False
    )
```

time: 263 us -> 185 us (0.70)
  waiting for transfers between devices: 138 us -> 0.75 us
  blocking collectives: 34.6 us -> 132 us
  loops' own time: 29.9 us -> 0 us
  local copies, waits for them, and re-layouts: 30.9 us -> 3.77 us
  starting transfers between devices: 0.07 us -> 15.5 us
  Pallas kernels: 0 us -> 13.2 us
  other arithmetic: 9.57 us -> 3.42 us
  matrix products: 5.76 us -> 0 us
    all_gather x2 -> x1, waiting for transfers between devices: 137 us -> 0.01 us  [on_device(): lax.all_gather(out_weight, ('z', 'core'), axis=0, tiled=False)]
    all_gather x0 -> x2, blocking collectives: none -> 95.8 us  [the longest x1 67.3 us: on_device(): keys_a = lax.all_gather(keys_here, 'z', axis=0, tiled=False)]
    another operation x9 -> x0, loops' own time: 29.9 us -> none  [the longest x1 29.7 us: on_device(): final_state, unused_out = lax.scan(step_block, start_state, blocks)]
    gather x3 -> x0, local copies, waits for them, and re-layouts: 24.2 us -> none  [the longest x2 23 us: on_device(): jnp.take(doc_ids, positions, axis=0).reshape(block_count, block_rows)]
    ppermute x0 -> x2, starting transfers between devices: none -> 15.5 us  [the longest x1 8.35 us: on_device(): keys_b = lax.ppermute(keys_a, 'core', swap)]
    pallas_call x0 -> x2, Pallas kernels: none -> 13.2 us  [the longest x1 8.29 us: on_device(): pl.pallas_call(functools.partial(project, share), grid=(members,), out_sh...]
    dot_general x3 -> x0, matrix products: 5.76 us -> none  [the longest x1 4.66 us: on_device(): jnp.dot(attention, lax.all_gather(out_weight, 'ctx', axis=1, tiled=True),...]
    reduce_max x8 -> x0, other arithmetic: 5.52 us -> none  [step_block(): jnp.max(block[2]) >= first_doc]
  transfers between devices with their start and end apart: 2 -> 3, of which waited for: 2 -> 0; matrix products, arithmetic and copies ran while one was open for 14% -> 3% of each run, Pallas kernels for 0% -> 3%
where the time goes in v1:
time: 185 us
  blocking collectives  132 us (71%)
  between operations  16.2 us (9%)
  starting transfers between devices  15.5 us (8%)
  Pallas kernels  13.2 us (7%)
  local copies, waits for them, and re-layouts  3.77 us (2%)
  other arithmetic  3.42 us (2%)
    all_gather x1, blocking collectives, on_device(): keys_a = lax.all_gather(keys_here, 'z', axis=0, tiled=False)  67.3 us
    all_to_all x1, blocking collectives, on_device(): lax.all_to_all(terms, 'tp', split_axis=0, concat_axis=0, tiled=True)  36.1 us
    all_gather x1, blocking collectives, on_device(): values_a = lax.all_gather(value_matrix, 'z', axis=0, tiled=False)  28.4 us
    ppermute x1, starting transfers between devices, on_device(): keys_b = lax.ppermute(keys_a, 'core', swap)  8.35 us
    pallas_call x1, Pallas kernels, on_device(): pl.pallas_call(functools.partial(project, share), grid=(members,), out_sh...  8.29 us
    ppermute x1, starting transfers between devices, on_device(): values_b = lax.ppermute(values_a, 'core', swap)  7.19 us
    pallas_call x1, Pallas kernels, on_device(): pl.pallas_call(functools.partial(attend, query_heads), out_shape=jax.Shap...  4.9 us
  transfers between devices with their start and end apart: 3, of which 0 were waited for; matrix products, arithmetic and copies ran while one was open for 3% of the time, Pallas kernels for 3%

profile of v1, /device:TPU:65, one launch (start us, length us, event | category | flops | bytes accessed | tf_op | source)
XLA Modules:
  0.0 184.7 jit_solution(15372599784641396918)
XLA Ops:
  6.5 0.0 copy-start.3
  6.5 0.0 copy-start.4
  6.6 0.0 copy-start.2
  6.6 0.0 all-gather.5.cloned.1.call-start
  6.6 0.7 all-gather.5.cloned.1.call-update
  7.3 0.9 copy.8
  8.2 0.2 fusion.5
  8.5 67.3 %all-gather = bf16[2048,1,128]{0,2,1:T(8,128)(2,1)S(1)} all-gather(bf16[128,1,128]{0,2,1:T(8,128)(2,1)S(1)} %pad_maximum_fusion.1), channel_id=2, replica_groups=mesh['groups'=2,'z'=16,'core'=2,'tp'=8] {'z'}, dimensions={0}, use_global_device_ids=true | all-gather | bytes 557056 | tf_op jit(solution)/shard_map/all_gather | solution.py:102
  75.8 0.3 copy.9
  76.1 0.0 copy-start
  76.1 8.4 %collective-permute-start = (bf16[16,128,128]{2,1,0:T(8,128)(2,1)S(1)}, bf16[16,128,128]{2,1,0:T(8,128)(2,1)S(1)}, u32[]{:S(2)}, u32[]{:S(2)}) collective-permute-start(bf16[16,128,128]{2,1,0:T(8,128)(2,1)S(1)} %bitcast.19), channel_id=1, source_target_pairs={{0,8},{8,0},{1,9},{9,1},{2,10},{10,2},{3,11},{11,3},{4,12},{12,4},... | collective-permute-start | bytes 1572872 | tf_op jit(solution)/shard_map/ppermute | solution.py:103
  84.4 0.0 copy-done.3
  84.5 28.4 %all-gather.1 = bf16[2048,128]{1,0:T(8,128)(2,1)S(1)} all-gather(bf16[128,128]{1,0:T(8,128)(2,1)S(1)} %copy-done.3), channel_id=3, replica_groups=mesh['groups'=2,'z'=16,'core'=2,'tp'=8] {'z'}, dimensions={0}, use_global_device_ids=true | all-gather | bytes 557056 | tf_op jit(solution)/shard_map/all_gather | solution.py:104
  112.9 0.0 copy-start.1
  112.9 7.2 %collective-permute-start.1 = (bf16[16,128,128]{2,1,0:T(8,128)(2,1)S(1)}, bf16[16,128,128]{2,1,0:T(8,128)(2,1)S(1)}, u32[]{:S(2)}, u32[]{:S(2)}) collective-permute-start(bf16[16,128,128]{2,1,0:T(8,128)(2,1)S(1)} %bitcast.21), channel_id=1, source_target_pairs={{0,8},{8,0},{1,9},{9,1},{2,10},{10,2},{3,11},{11,3},{4,12},{12,4},... | collective-permute-start | bytes 1572872 | tf_op jit(solution)/shard_map/ppermute | solution.py:105
  120.1 0.0 copy-done.4
  120.1 0.1 dynamic_slice.3
  120.2 0.3 multiply_cosine_fusion
  120.5 0.0 copy-done.2
  120.5 0.4 convert_reduce_fusion
  120.9 0.6 reduce_min.9
  124.1 0.1 copy.11
  124.2 0.3 subtract_convert_fusion
  124.5 0.0 copy-done
  124.5 0.1 pad_maximum_fusion
  124.7 0.0 copy-done.1
  124.7 0.8 copy.14
  125.4 0.7 copy.10.start_ref
  126.2 0.6 pad_add_fusion.info
  126.8 0.0 collective-permute-done.kb_ref
  126.8 0.0 copy-start.5
  126.8 0.0 collective-permute-done.1.vb_ref
  126.8 0.0 copy-start.6
  126.8 0.8 copy-done.5
  127.6 0.2 copy-done.6
  127.8 4.9 %attend.1.a_ref = bf16[128,1024]{1,0:T(8,128)(2,1)} custom-call(s32[2]{0:T(128)} %pad_add_fusion.info, s32[128,1]{1,0:T(8,128)} %copy.10.start_ref, bf16[128,1024]{1,0:T(8,128)(2,1)} %bitcast.23, bf16[16,128,128]{2,1,0:T(8,128)(2,1)} %bitcast.20, bf16[16,128,128]{2,1,0:T(8,128)(2,1)} %copy-done.5, bf16[16,128,128]{2,1,0:T(8,128)(2,1)} %bitcast.22, ...), custom_call_target="tpu_custom_call" | custom-call | flops 2000000000 | bytes 3000000 | tf_op jit(solution)/shard_map/attend/pallas_call | solution.py:112
  132.7 0.0 all-gather.5.cloned.1.call-done
  132.7 8.3 %project.1 = bf16[8,128,512]{2,1,0:T(8,128)(2,1)} custom-call(bf16[128,1024]{1,0:T(8,128)(2,1)} %attend.1.a_ref, bf16[32,1024,128]{2,1,0:T(8,128)(2,1)} %bitcast.16), custom_call_target="tpu_custom_call" | custom-call | flops 1000000000 | bytes 10000000 | tf_op jit(solution)/shard_map/project/pallas_call | solution.py:127
  140.9 36.1 %all_to_all.5 = bf16[8,128,512]{2,1,0:T(8,128)(2,1)S(1)} all-to-all(bf16[8,128,512]{2,1,0:T(8,128)(2,1)} %project.1), channel_id=1, replica_groups=mesh['groups'=2,'z'=16,'core'=2,'tp'=8] {'tp'}, dimensions={0} | all-to-all | bytes 2097152 | tf_op jit(solution)/shard_map/all_to_all | solution.py:139
  177.0 0.8 reduce_sum.22
  (5 shorter events, 0.1 us)
Async XLA Ops:
  6.5 77.9 %copy-start.3 = (bf16[128,128]{1,0:T(8,128)(2,1)S(1)}, bf16[128,128]{1,0:T(8,128)(2,1)}, u32[]{:S(2)}) copy-start(bf16[128,128]{1,0:T(8,128)(2,1)} %param.7) | copy-start | bytes 98308
  6.5 113.5 %copy-start.4 = (s32[4096]{0:T(1024)S(1)}, s32[4096]{0:T(1024)}, u32[]{:S(2)}) copy-start(s32[4096]{0:T(1024)} %param.8) | copy-start | bytes 49156
  6.6 113.9 %copy-start.2 = (bf16[128,1024]{1,0:T(8,128)(2,1)S(1)}, bf16[128,1024]{1,0:T(8,128)(2,1)}, u32[]{:S(2)}) copy-start(bf16[128,1024]{1,0:T(8,128)(2,1)} %param.5) | copy-start | bytes 786436
  6.6 126.1 %all-gather.5.cloned.1.call-start = ((), (), s32[]{:S(2)}) async-start(), calls=%async_computation.1 | async-start | bytes 8650752 | tf_op jit(solution)/shard_map/all_gather | solution.py:97
  76.1 48.4 %copy-start = (bf16[2048,1,128]{2,0,1:T(8,128)(2,1)}, bf16[2048,1,128]{2,0,1:T(8,128)(2,1)S(1)}, u32[]{:S(2)}) copy-start(bf16[2048,1,128]{2,0,1:T(8,128)(2,1)S(1)} %copy.9) | copy-start | bytes 1572868
  76.1 50.7 %collective-permute-start = (bf16[16,128,128]{2,1,0:T(8,128)(2,1)S(1)}, bf16[16,128,128]{2,1,0:T(8,128)(2,1)S(1)}, u32[]{:S(2)}, u32[]{:S(2)}) collective-permute-start(bf16[16,128,128]{2,1,0:T(8,128)(2,1)S(1)} %bitcast.19), channel_id=1, source_target_pairs={{0,8},{8,0},{1,9},{9,1},{2,10},{10,2},{3,11},{11,3},{4,12},{12,4},... | collective-permute-start | bytes 1572872 | tf_op jit(solution)/shard_map/ppermute | solution.py:103
  112.9 11.8 %copy-start.1 = (bf16[2048,128]{1,0:T(8,128)(2,1)}, bf16[2048,128]{1,0:T(8,128)(2,1)S(1)}, u32[]{:S(2)}) copy-start(bf16[2048,128]{1,0:T(8,128)(2,1)S(1)} %all-gather.1) | copy-start | bytes 1572868
  112.9 13.9 %collective-permute-start.1 = (bf16[16,128,128]{2,1,0:T(8,128)(2,1)S(1)}, bf16[16,128,128]{2,1,0:T(8,128)(2,1)S(1)}, u32[]{:S(2)}, u32[]{:S(2)}) collective-permute-start(bf16[16,128,128]{2,1,0:T(8,128)(2,1)S(1)} %bitcast.21), channel_id=1, source_target_pairs={{0,8},{8,0},{1,9},{9,1},{2,10},{10,2},{3,11},{11,3},{4,12},{12,4},... | collective-permute-start | bytes 1572872 | tf_op jit(solution)/shard_map/ppermute | solution.py:105
  126.8 0.8 copy-start.5
  126.8 1.0 copy-start.6
Sparse Core Ops, SparseCore 0:
  9.5 119.5 all-gather.4

commit v2 on v1

v2 whole, which is shorter than its diff:
```python
import functools
import math

import jax
import jax.numpy as jnp
from jax import lax
from jax.experimental import pallas as pl
from jax.experimental.pallas import tpu as pltpu
from jax.sharding import Mesh
from jax.sharding import PartitionSpec as P

HEAD_SIZE = 128
CORES = 2
DOCS = 6


rope_base = 1000000.0


def rotary_tables(token_positions):
    half_dim = HEAD_SIZE // 2
    lane = jnp.arange(HEAD_SIZE, dtype=jnp.int32)
    power = -(lane % half_dim).astype(jnp.float32) * (2.0 / HEAD_SIZE)
    angles = token_positions.astype(jnp.float32)[:, None] * jnp.power(jnp.float32(rope_base), power)
    return jnp.cos(angles), jnp.where(lane < half_dim, -1.0, 1.0) * jnp.sin(angles)


def prepare(heads, cosine_ref, sine_ref, q_ref, k_ref, v_ref, q_out, k_out, v_out):
    cosine, sine = cosine_ref[...], sine_ref[...]

    def turned(x):
        x = x.astype(jnp.float32)
        return (x * cosine + pltpu.roll(x, HEAD_SIZE // 2, 1) * sine).astype(jnp.bfloat16)

    k_out[...] = turned(k_ref[...])
    v_out[...] = v_ref[...].astype(jnp.float32).T.astype(jnp.bfloat16)
    for h in range(heads):
        at = slice(h * HEAD_SIZE, (h + 1) * HEAD_SIZE)
        q_out[:, at] = turned(q_ref[:, at])


def attend(heads, info, doc_ref, q_ref, ka_ref, kb_ref, va_ref, vb_ref, out_ref, m_ref, l_ref, acc_ref):
    rows = q_ref.shape[0]
    ctx = info[0]
    core = lax.rem(ctx, CORES)
    scale = HEAD_SIZE**-0.5 * math.log2(math.e)
    m_ref[...] = jnp.full(m_ref.shape, -1e30, jnp.float32)
    l_ref[...] = jnp.zeros(l_ref.shape, jnp.float32)
    acc_ref[...] = jnp.zeros(acc_ref.shape, jnp.float32)
    width = CORES * rows
    key = lax.broadcasted_iota(jnp.int32, (width, rows), 0)
    given = ctx * rows + lax.broadcasted_iota(jnp.int32, (width, rows), 1)
    mine = key < rows
    docs, here = doc_ref[...], doc_ref[pl.ds(ctx, 1), :]
    first = jnp.zeros(here.shape, jnp.int32)
    for d in range(1, DOCS):
        before = jnp.sum((docs < d).astype(jnp.int32), keepdims=True)
        first = first + jnp.where(here == d, before, 0)
    first_pair = lax.div(jnp.min(first), width)

    def one_pair(step, carry):
        pair = lax.div(ctx, CORES) - step
        own = (pair * CORES + core) * rows
        other = (pair * CORES + (1 - core)) * rows - rows
        position = key + jnp.where(mine, own, other)
        allowed = (position >= first) & (position <= given)
        keys = jnp.concatenate([ka_ref[pair], kb_ref[pair]], 0)
        values = jnp.concatenate([va_ref[pair], vb_ref[pair]], 1)
        for h in range(heads):
            q = q_ref[:, h * HEAD_SIZE : (h + 1) * HEAD_SIZE]
            scores = lax.dot_general(
                keys, q, (((1,), (1,)), ((), ())), preferred_element_type=jnp.float32
            )
            scores = jnp.where(allowed, scores, -1e30)
            old = m_ref[h]
            new = jnp.maximum(old, jnp.max(scores, 0, keepdims=True))
            weights = jnp.exp2((scores - new) * scale)
            factor = jnp.exp2((old - new) * scale)
            m_ref[h] = new
            l_ref[h] = l_ref[h] * factor + jnp.sum(weights, 0, keepdims=True)
            acc_ref[h] = acc_ref[h] * factor + jnp.dot(
                values, weights.astype(jnp.bfloat16), preferred_element_type=jnp.float32
            )
        return carry

    lax.fori_loop(0, lax.div(ctx, CORES) - first_pair + 1, one_pair, 0)
    for h in range(heads):
        out_ref[:, h * HEAD_SIZE : (h + 1) * HEAD_SIZE] = (
            (acc_ref[h] / l_ref[h]).T.astype(jnp.bfloat16)
        )


def project(count, a_ref, w_ref, out_ref):
    weights = jnp.concatenate([w_ref[i] for i in range(count)], 1)
    out_ref[0] = jnp.dot(a_ref[...], weights, preferred_element_type=jnp.float32).astype(
        jnp.bfloat16
    )


def on_device(query_matrix, key_matrix, value_matrix, doc_ids, out_weight):
    tok_rows = query_matrix.shape[0]
    query_heads = query_matrix.shape[1] // HEAD_SIZE
    members = lax.axis_size("tp")
    ctx_index = lax.axis_index("z") * CORES + lax.axis_index("core")
    weight_blocks = lax.all_gather(out_weight, ("z", "core"), axis=0, tiled=False)
    given_pos = ctx_index * tok_rows + jnp.arange(tok_rows, dtype=jnp.int32)
    vmem = pl.BlockSpec(memory_space=pltpu.VMEM)
    queries, keys_here, values_here = pl.pallas_call(
        functools.partial(prepare, query_heads),
        out_shape=(
            jax.ShapeDtypeStruct(query_matrix.shape, jnp.bfloat16),
            jax.ShapeDtypeStruct(key_matrix.shape, jnp.bfloat16),
            jax.ShapeDtypeStruct(value_matrix.shape[::-1], jnp.bfloat16),
        ),
        in_specs=[vmem] * 5,
        out_specs=(vmem,) * 3,
        compiler_params=pltpu.CompilerParams(vmem_limit_bytes=16 * 2**20),
        cost_estimate=pl.CostEstimate(flops=10**6, bytes_accessed=10**6, transcendentals=0),
        name="prepare",
    )(*rotary_tables(given_pos), query_matrix, key_matrix, value_matrix)
    swap = [(i, CORES - 1 - i) for i in range(CORES)]
    keys_a = lax.all_gather(keys_here, "z", axis=0, tiled=False)
    keys_b = lax.ppermute(keys_a, "core", swap)
    values_a = lax.all_gather(values_here, "z", axis=0, tiled=False)
    values_b = lax.ppermute(values_a, "core", swap)
    info = ctx_index.astype(jnp.int32).reshape(1)
    docs = doc_ids.reshape(-1, tok_rows)
    attention = pl.pallas_call(
        functools.partial(attend, query_heads),
        out_shape=jax.ShapeDtypeStruct((tok_rows, query_heads * HEAD_SIZE), jnp.bfloat16),
        in_specs=[pl.BlockSpec(memory_space=pltpu.SMEM)] + [vmem] * 6,
        out_specs=vmem,
        scratch_shapes=[
            pltpu.VMEM((query_heads, 1, tok_rows), jnp.float32),
            pltpu.VMEM((query_heads, 1, tok_rows), jnp.float32),
            pltpu.VMEM((query_heads, tok_rows, HEAD_SIZE), jnp.float32),
        ],
        cost_estimate=pl.CostEstimate(flops=2 * 10**9, bytes_accessed=3 * 10**6, transcendentals=10**6),
        compiler_params=pltpu.CompilerParams(vmem_limit_bytes=16 * 2**20),
        name="attend",
    )(info, docs, queries, keys_a, keys_b, values_a, values_b)
    blocks, depth, width = weight_blocks.shape
    share = blocks // members
    terms = pl.pallas_call(
        functools.partial(project, share),
        grid=(members,),
        out_shape=jax.ShapeDtypeStruct((members, tok_rows, share * width), jnp.bfloat16),
        in_specs=[
            pl.BlockSpec((tok_rows, depth), lambda i: (0, 0)),
            pl.BlockSpec((share, depth, width), lambda i: (i, 0, 0)),
        ],
        out_specs=pl.BlockSpec((1, tok_rows, share * width), lambda i: (i, 0, 0)),
        cost_estimate=pl.CostEstimate(flops=10**9, bytes_accessed=10**7, transcendentals=0),
        name="project",
    )(attention, weight_blocks)
    arrived = lax.all_to_all(terms, "tp", split_axis=0, concat_axis=0, tiled=True)
    return arrived.astype(jnp.float32).sum(axis=0).astype(jnp.bfloat16)


def solution(mesh):
    groups, ctx, tp = mesh.devices.shape
    fine = Mesh(mesh.devices.reshape(groups, ctx // CORES, CORES, tp), ("groups", "z", "core", "tp"))
    tokens = ("groups", "z", "core")
    in_specs = (P(tokens, "tp"), P(tokens, "tp"), P(tokens, "tp"), P("groups"), P("tp", ("z", "core")))
    return jax.shard_map(
        on_device, mesh=fine, in_specs=in_specs, out_specs=P(tokens, "tp"), check_vma=False
    )
```

time: 185 us -> 180 us (0.973)
  waiting for transfers between devices: 0.75 us -> 4.63 us
  Pallas kernels: 13.2 us -> 9.37 us
  between operations: 16.2 us -> 13.5 us
  other arithmetic: 3.42 us -> 1.14 us
    pallas_call x1, Pallas kernels: 4.9 us -> 1.31 us  [on_device(): pl.pallas_call(functools.partial(attend, query_heads), out_shape=jax.Shap...]
    all_gather x1, waiting for transfers between devices: 0.01 us -> 2.37 us  [on_device(): lax.all_gather(out_weight, ('z', 'core'), axis=0, tiled=False)]
    unnamed x17 -> x10, local copies, waits for them, and re-layouts: 2.68 us -> 3.87 us
  transfers between devices with their start and end apart: 3 -> 3, of which waited for: 0 -> 2; matrix products, arithmetic and copies ran while one was open for 3% -> 0% of each run, Pallas kernels for 3% -> 1%
where the time goes in v2:
time: 180 us; the launch traced here: 179 us
  blocking collectives  133 us (74%)
  starting transfers between devices  14.1 us (8%)
  between operations  13.5 us (8%)
  Pallas kernels  9.37 us (5%)
  waiting for transfers between devices  4.63 us (3%)
  local copies, waits for them, and re-layouts  3.87 us (2%)
    all_gather x1, blocking collectives, on_device(): keys_a = lax.all_gather(keys_here, 'z', axis=0, tiled=False)  68.3 us
    all_to_all x1, blocking collectives, on_device(): lax.all_to_all(terms, 'tp', split_axis=0, concat_axis=0, tiled=True)  35.7 us
    all_gather x1, blocking collectives, on_device(): values_a = lax.all_gather(values_here, 'z', axis=0, tiled=False)  28.6 us
    pallas_call x1, Pallas kernels, on_device(): pl.pallas_call(functools.partial(project, share), grid=(members,), out_sh...  7.86 us
    ppermute x1, starting transfers between devices, on_device(): keys_b = lax.ppermute(keys_a, 'core', swap)  7.79 us
    ppermute x1, starting transfers between devices, on_device(): values_b = lax.ppermute(values_a, 'core', swap)  6.35 us
    unnamed x10, local copies, waits for them, and re-layouts  3.87 us
  transfers between devices with their start and end apart: 3, of which 2 were waited for; matrix products, arithmetic and copies ran while one was open for 0% of the time, Pallas kernels for 1%

profile of v2, /device:TPU:65, one launch (start us, length us, event | category | flops | bytes accessed | tf_op | source)
XLA Modules:
  0.0 179.3 jit_solution(5457385412457073387)
XLA Ops:
  6.5 0.0 all-gather.5.cloned.1.call-start
  6.6 0.7 all-gather.5.cloned.1.call-update
  7.3 0.3 fusion
  7.7 0.0 copy-start.1
  7.7 0.9 copy-done.1
  8.6 0.0 copy-start.2
  8.6 0.8 copy-done.2
  9.4 0.0 copy-start.3
  9.4 0.8 copy-done.3
  10.1 0.2 prepare.1
  10.3 68.3 %all-gather = bf16[2048,128]{1,0:T(8,128)(2,1)S(1)} all-gather(bf16[128,128]{1,0:T(8,128)(2,1)S(1)} %get-tuple-element.9), channel_id=2, replica_groups=mesh['groups'=2,'z'=16,'core'=2,'tp'=8] {'z'}, dimensions={0}, use_global_device_ids=true | all-gather | bytes 557056 | tf_op jit(solution)/shard_map/all_gather | solution.py:122
  78.6 7.8 %collective-permute-start = (bf16[16,128,128]{2,1,0:T(8,128)(2,1)S(1)}, bf16[16,128,128]{2,1,0:T(8,128)(2,1)S(1)}, u32[]{:S(2)}, u32[]{:S(2)}) collective-permute-start(bf16[16,128,128]{2,1,0:T(8,128)(2,1)S(1)} %bitcast.5), channel_id=1, source_target_pairs={{0,8},{8,0},{1,9},{9,1},{2,10},{10,2},{3,11},{11,3},{4,12},{12,4},... | collective-permute-start | bytes 1572872 | tf_op jit(solution)/shard_map/ppermute | solution.py:123
  86.4 28.6 %all-gather.1 = bf16[2048,128]{1,0:T(8,128)(2,1)S(1)} all-gather(bf16[128,128]{1,0:T(8,128)(2,1)S(1)} %get-tuple-element.10), channel_id=3, replica_groups=mesh['groups'=2,'z'=16,'core'=2,'tp'=8] {'z'}, dimensions={0}, use_global_device_ids=true | all-gather | bytes 557056 | tf_op jit(solution)/shard_map/all_gather | solution.py:124
  115.0 6.3 %collective-permute-start.1 = (bf16[16,128,128]{2,1,0:T(8,128)(2,1)S(1)}, bf16[16,128,128]{2,1,0:T(8,128)(2,1)S(1)}, u32[]{:S(2)}, u32[]{:S(2)}) collective-permute-start(bf16[16,128,128]{2,1,0:T(8,128)(2,1)S(1)} %bitcast.7), channel_id=1, source_target_pairs={{0,8},{8,0},{1,9},{9,1},{2,10},{10,2},{3,11},{11,3},{4,12},{12,4},... | collective-permute-start | bytes 1572872 | tf_op jit(solution)/shard_map/ppermute | solution.py:125
  121.4 0.0 collective-permute-done.kb_ref
  121.4 1.5 collective-permute-done.1.vb_ref
  122.9 0.0 copy-start.4
  122.9 0.7 copy-done.4
  123.6 1.3 attend.1.a_ref
  124.9 0.0 copy-start
  124.9 0.7 copy-done
  125.6 2.4 %all-gather.5.cloned.1.call-done = bf16[32768,128]{1,0:T(8,128)(2,1)} async-done(((bf16[1024,128]{1,0:T(8,128)(2,1)}), bf16[32768,128]{1,0:T(8,128)(2,1)}) %all-gather.5.cloned.1.call-update) | async-done | bytes 8388624 | tf_op jit(solution)/shard_map/all_gather | solution.py:105
  128.0 7.9 %project.1 = bf16[8,128,512]{2,1,0:T(8,128)(2,1)} custom-call(bf16[128,1024]{1,0:T(8,128)(2,1)} %copy-done, bf16[32,1024,128]{2,1,0:T(8,128)(2,1)} %bitcast.10), custom_call_target="tpu_custom_call" | custom-call | flops 1000000000 | bytes 10000000 | tf_op jit(solution)/shard_map/project/pallas_call | solution.py:144
  135.9 35.7 %all_to_all.5 = bf16[8,128,512]{2,1,0:T(8,128)(2,1)S(1)} all-to-all(bf16[8,128,512]{2,1,0:T(8,128)(2,1)} %project.1), channel_id=1, replica_groups=mesh['groups'=2,'z'=16,'core'=2,'tp'=8] {'tp'}, dimensions={0} | all-to-all | bytes 2097152 | tf_op jit(solution)/shard_map/all_to_all | solution.py:156
  171.6 0.8 reduce_sum.12
  (2 shorter events, 0.0 us)
Async XLA Ops:
  6.5 121.5 %all-gather.5.cloned.1.call-start = ((), (), s32[]{:S(2)}) async-start(), calls=%async_computation.1 | async-start | bytes 8650752 | tf_op jit(solution)/shard_map/all_gather | solution.py:105
  7.7 1.0 copy-start.1
  8.6 0.8 copy-start.2
  9.4 0.8 copy-start.3
  78.6 42.8 %collective-permute-start = (bf16[16,128,128]{2,1,0:T(8,128)(2,1)S(1)}, bf16[16,128,128]{2,1,0:T(8,128)(2,1)S(1)}, u32[]{:S(2)}, u32[]{:S(2)}) collective-permute-start(bf16[16,128,128]{2,1,0:T(8,128)(2,1)S(1)} %bitcast.5), channel_id=1, source_target_pairs={{0,8},{8,0},{1,9},{9,1},{2,10},{10,2},{3,11},{11,3},{4,12},{12,4},... | collective-permute-start | bytes 1572872 | tf_op jit(solution)/shard_map/ppermute | solution.py:123
  115.0 7.9 %collective-permute-start.1 = (bf16[16,128,128]{2,1,0:T(8,128)(2,1)S(1)}, bf16[16,128,128]{2,1,0:T(8,128)(2,1)S(1)}, u32[]{:S(2)}, u32[]{:S(2)}) collective-permute-start(bf16[16,128,128]{2,1,0:T(8,128)(2,1)S(1)} %bitcast.7), channel_id=1, source_target_pairs={{0,8},{8,0},{1,9},{9,1},{2,10},{10,2},{3,11},{11,3},{4,12},{12,4},... | collective-permute-start | bytes 1572872 | tf_op jit(solution)/shard_map/ppermute | solution.py:125
  122.9 0.7 copy-start.4
  124.9 0.7 copy-start
Sparse Core Ops, SparseCore 0:
  9.5 118.4 all-gather.4

commit v3 on v2

v3 whole, which is shorter than its diff:
```python
import functools
import math

import jax
import jax.numpy as jnp
from jax import lax
from jax.experimental import pallas as pl
from jax.experimental.pallas import tpu as pltpu
from jax.sharding import Mesh
from jax.sharding import PartitionSpec as P

HEAD_SIZE = 128
CORES = 2
DOCS = 6
MAX_DOC = 2048


rope_base = 1000000.0


def rotary_tables(token_positions):
    half_dim = HEAD_SIZE // 2
    lane = jnp.arange(HEAD_SIZE, dtype=jnp.int32)
    power = -(lane % half_dim).astype(jnp.float32) * (2.0 / HEAD_SIZE)
    angles = token_positions.astype(jnp.float32)[:, None] * jnp.power(jnp.float32(rope_base), power)
    return jnp.cos(angles), jnp.where(lane < half_dim, -1.0, 1.0) * jnp.sin(angles)


def prepare(heads, cosine_ref, sine_ref, q_ref, k_ref, v_ref, q_out, kv_out):
    cosine, sine = cosine_ref[...], sine_ref[...]

    def turned(x):
        x = x.astype(jnp.float32)
        return (x * cosine + pltpu.roll(x, HEAD_SIZE // 2, 1) * sine).astype(jnp.bfloat16)

    kv_out[0] = turned(k_ref[...])
    kv_out[1] = v_ref[...].astype(jnp.float32).T.astype(jnp.bfloat16)
    for h in range(heads):
        at = slice(h * HEAD_SIZE, (h + 1) * HEAD_SIZE)
        q_out[:, at] = turned(q_ref[:, at])


def attend(heads, info, doc_ref, q_ref, a_ref, b_ref, out_ref, m_ref, l_ref, acc_ref):
    rows = q_ref.shape[0]
    line = a_ref.shape[0]
    ctx = info[0]
    core = lax.rem(ctx, CORES)
    chip = lax.div(ctx, CORES)
    scale = HEAD_SIZE**-0.5 * math.log2(math.e)
    m_ref[...] = jnp.full(m_ref.shape, -1e30, jnp.float32)
    l_ref[...] = jnp.zeros(l_ref.shape, jnp.float32)
    acc_ref[...] = jnp.zeros(acc_ref.shape, jnp.float32)
    width = CORES * rows
    key = lax.broadcasted_iota(jnp.int32, (width, rows), 0)
    given = ctx * rows + lax.broadcasted_iota(jnp.int32, (width, rows), 1)
    mine = key < rows
    docs, here = doc_ref[...], doc_ref[pl.ds(ctx, 1), :]
    first = jnp.zeros(here.shape, jnp.int32)
    for d in range(1, DOCS):
        before = jnp.sum((docs < d).astype(jnp.int32), keepdims=True)
        first = first + jnp.where(here == d, before, 0)
    first_chip = lax.div(jnp.min(first), width)

    def one_chip(step, carry):
        at = chip - step
        own = (at * CORES + core) * rows
        other = (at * CORES + (1 - core)) * rows - rows
        position = key + jnp.where(mine, own, other)
        allowed = (position >= first) & (position <= given)
        member, back = lax.rem(at, line), lax.div(chip, line) - lax.div(at, line)
        keys = jnp.concatenate([a_ref[member, back, 0], b_ref[member, back, 0]], 0)
        values = jnp.concatenate([a_ref[member, back, 1], b_ref[member, back, 1]], 1)
        for h in range(heads):
            q = q_ref[:, h * HEAD_SIZE : (h + 1) * HEAD_SIZE]
            scores = lax.dot_general(
                keys, q, (((1,), (1,)), ((), ())), preferred_element_type=jnp.float32
            )
            scores = jnp.where(allowed, scores, -1e30)
            old = m_ref[h]
            new = jnp.maximum(old, jnp.max(scores, 0, keepdims=True))
            weights = jnp.exp2((scores - new) * scale)
            factor = jnp.exp2((old - new) * scale)
            m_ref[h] = new
            l_ref[h] = l_ref[h] * factor + jnp.sum(weights, 0, keepdims=True)
            acc_ref[h] = acc_ref[h] * factor + jnp.dot(
                values, weights.astype(jnp.bfloat16), preferred_element_type=jnp.float32
            )
        return carry

    lax.fori_loop(0, chip - first_chip + 1, one_chip, 0)
    for h in range(heads):
        out_ref[:, h * HEAD_SIZE : (h + 1) * HEAD_SIZE] = (
            (acc_ref[h] / l_ref[h]).T.astype(jnp.bfloat16)
        )


def project(count, level_ref, own_ref, other_ref, *refs):
    out_ref = refs[count]
    rows = own_ref.shape[0]
    weights = jnp.concatenate([w_ref[0] for w_ref in refs[:count]], 1)
    for i, a_ref in enumerate((own_ref, other_ref)):
        out_ref[0, i * rows : (i + 1) * rows] = jnp.dot(
            a_ref[...], weights, preferred_element_type=jnp.float32
        ).astype(jnp.bfloat16)


def total(terms_ref, kept_ref, sent_ref):
    rows = kept_ref.shape[0]
    for i, out_ref in enumerate((kept_ref, sent_ref)):
        at = slice(i * rows, (i + 1) * rows)
        out_ref[...] = jnp.sum(terms_ref[:, at].astype(jnp.float32), 0).astype(jnp.bfloat16)


def weave(count, core, kept_ref, given_ref, out_ref):
    width = kept_ref.shape[1] // count
    even = core[0] == 0
    for j in range(count):
        kept, given = (r[:, j * width : (j + 1) * width] for r in (kept_ref, given_ref))
        at = j * CORES * width
        out_ref[:, at : at + width] = jnp.where(even, kept, given)
        out_ref[:, at + width : at + CORES * width] = jnp.where(even, given, kept)


def on_device(query_matrix, key_matrix, value_matrix, doc_ids, out_weight):
    tok_rows = query_matrix.shape[0]
    query_heads = query_matrix.shape[1] // HEAD_SIZE
    members = lax.axis_size("tp")
    lines, line = lax.axis_size("far"), lax.axis_size("near")
    core = lax.axis_index("core")
    my_line = lax.axis_index("far")
    ctx_index = (my_line * line + lax.axis_index("near")) * CORES + core
    weight_blocks = lax.all_gather(out_weight, ("far", "near"), axis=0, tiled=False)
    given_pos = ctx_index * tok_rows + jnp.arange(tok_rows, dtype=jnp.int32)
    vmem = pl.BlockSpec(memory_space=pltpu.VMEM)
    small = pltpu.CompilerParams(vmem_limit_bytes=16 * 2**20)
    queries, here = pl.pallas_call(
        functools.partial(prepare, query_heads),
        out_shape=(
            jax.ShapeDtypeStruct(query_matrix.shape, jnp.bfloat16),
            jax.ShapeDtypeStruct((2,) + key_matrix.shape, jnp.bfloat16),
        ),
        in_specs=[vmem] * 5,
        out_specs=(vmem,) * 2,
        compiler_params=small,
        cost_estimate=pl.CostEstimate(flops=10**6, bytes_accessed=10**6, transcendentals=0),
        name="prepare",
    )(*rotary_tables(given_pos), query_matrix, key_matrix, value_matrix)
    swap = [(i, CORES - 1 - i) for i in range(CORES)]
    far = lax.all_gather(here, "far", axis=0, tiled=False)
    back = min(lines, 1 + -(-(MAX_DOC - 1) // (line * CORES * tok_rows)))
    wanted = jnp.stack(
        [
            lax.dynamic_index_in_dim(far, (my_line - i) % lines, 0, keepdims=False)
            for i in range(back)
        ]
    )
    mine = lax.all_gather(wanted, "near", axis=0, tiled=False)
    theirs = lax.ppermute(mine, "core", swap)
    info = ctx_index.astype(jnp.int32).reshape(1)
    docs = doc_ids.reshape(-1, tok_rows)
    attention = pl.pallas_call(
        functools.partial(attend, query_heads),
        out_shape=jax.ShapeDtypeStruct((tok_rows, query_heads * HEAD_SIZE), jnp.bfloat16),
        in_specs=[pl.BlockSpec(memory_space=pltpu.SMEM)] + [vmem] * 4,
        out_specs=vmem,
        scratch_shapes=[
            pltpu.VMEM((query_heads, 1, tok_rows), jnp.float32),
            pltpu.VMEM((query_heads, 1, tok_rows), jnp.float32),
            pltpu.VMEM((query_heads, HEAD_SIZE, tok_rows), jnp.float32),
        ],
        cost_estimate=pl.CostEstimate(flops=2 * 10**9, bytes_accessed=3 * 10**6, transcendentals=10**6),
        compiler_params=small,
        name="attend",
    )(info, docs, queries, mine, theirs)
    level = lax.all_to_all(
        attention[: members * 8, :HEAD_SIZE].reshape(members, 8, HEAD_SIZE),
        "tp",
        split_axis=0,
        concat_axis=0,
        tiled=True,
    )
    attention_other = lax.ppermute(attention, "core", swap)
    blocks, depth, width = weight_blocks.shape
    share = blocks // members
    whole = pl.BlockSpec((tok_rows, depth), lambda i: (0, 0))
    terms = pl.pallas_call(
        functools.partial(project, share),
        grid=(members,),
        out_shape=jax.ShapeDtypeStruct((members, CORES * tok_rows, share * width), jnp.bfloat16),
        in_specs=[pl.BlockSpec(memory_space=pl.ANY), whole, whole]
        + [
            pl.BlockSpec((1, depth, width), lambda i, j=j: (i * share + j, 0, 0))
            for j in range(share)
        ],
        out_specs=pl.BlockSpec((1, CORES * tok_rows, share * width), lambda i: (i, 0, 0)),
        cost_estimate=pl.CostEstimate(flops=10**9, bytes_accessed=10**7, transcendentals=0),
        name="project",
    )(level, attention, attention_other, *[weight_blocks] * share)
    arrived = lax.all_to_all(terms, "tp", split_axis=0, concat_axis=0, tiled=True)
    half = jax.ShapeDtypeStruct((tok_rows, share * width), jnp.bfloat16)
    kept, sent = pl.pallas_call(
        total,
        out_shape=(half, half),
        in_specs=[vmem],
        out_specs=(vmem, vmem),
        compiler_params=small,
        name="total",
    )(arrived)
    given = lax.ppermute(sent, "core", swap)
    return pl.pallas_call(
        functools.partial(weave, share),
        out_shape=jax.ShapeDtypeStruct((tok_rows, share * CORES * width), jnp.bfloat16),
        in_specs=[pl.BlockSpec(memory_space=pltpu.SMEM), vmem, vmem],
        out_specs=vmem,
        compiler_params=small,
        name="weave",
    )(core.astype(jnp.int32).reshape(1), kept, given)


def solution(mesh):
    groups, ctx, tp = mesh.devices.shape
    near = math.gcd(ctx // CORES, 4)
    far = ctx // CORES // near
    names = ("groups", "far", "near", "core", "tp")
    fine = Mesh(mesh.devices.reshape(groups, far, near, CORES, tp), names)
    ctx_axes = ("far", "near", "core")
    tokens = ("groups",) + ctx_axes
    in_specs = (P(tokens, "tp"), P(tokens, "tp"), P(tokens, "tp"), P("groups"), P("tp", ctx_axes))
    return jax.shard_map(
        on_device, mesh=fine, in_specs=in_specs, out_specs=P(tokens, "tp"), check_vma=False
    )
```

time: 180 us -> 181 us (level)
  blocking collectives: 133 us -> 120 us
  starting transfers between devices: 14.1 us -> 22.4 us
  waiting for transfers between devices: 4.63 us -> 11.6 us
    all_gather x2, blocking collectives: 96.9 us -> 81 us  [the longest x1 48.4 us: on_device(): far = lax.all_gather(here, 'far', axis=0, tiled=False)]
    all_to_all x0 -> x1, blocking collectives: none -> 11.7 us  [on_device(): lax.all_to_all(attention[:members * 8, :HEAD_SIZE].reshape(members, 8, HE...]
    all_to_all x1, blocking collectives: 35.7 us -> 27.1 us  [on_device(): lax.all_to_all(terms, 'tp', split_axis=0, concat_axis=0, tiled=True)]
    ppermute x2 -> x3, starting transfers between devices: 14.1 us -> 22.4 us  [the longest x1 11.2 us: on_device(): given = lax.ppermute(sent, 'core', swap)]
    all_gather x1, waiting for transfers between devices: 2.37 us -> 8.08 us  [on_device(): lax.all_gather(out_weight, ('far', 'near'), axis=0, tiled=False)]
    unnamed x10 -> x12, local copies, waits for them, and re-layouts: 3.87 us -> 3.18 us
  transfers between devices with their start and end apart: 3 -> 4, of which waited for: 2 -> 3; matrix products, arithmetic and copies ran while one was open for 0% -> 0% of each run, Pallas kernels for 1% -> 1%
where the time goes in v3:
time: 181 us; the launch traced here: 180 us
  blocking collectives  120 us (66%)
  starting transfers between devices  22.4 us (12%)
  between operations  13.6 us (8%)
  waiting for transfers between devices  11.6 us (6%)
  Pallas kernels  9.44 us (5%)
  local copies, waits for them, and re-layouts  3.21 us (2%)
    all_gather x1, blocking collectives, on_device(): far = lax.all_gather(here, 'far', axis=0, tiled=False)  48.4 us
    all_gather x1, blocking collectives, on_device(): mine = lax.all_gather(wanted, 'near', axis=0, tiled=False)  32.6 us
    all_to_all x1, blocking collectives, on_device(): lax.all_to_all(terms, 'tp', split_axis=0, concat_axis=0, tiled=True)  27.1 us
    all_to_all x1, blocking collectives, on_device(): lax.all_to_all(attention[:members * 8, :HEAD_SIZE].reshape(members, 8, HE...  11.7 us
    ppermute x1, starting transfers between devices, on_device(): given = lax.ppermute(sent, 'core', swap)  11.2 us
    ppermute x1, starting transfers between devices, on_device(): theirs = lax.ppermute(mine, 'core', swap)  8.87 us
    all_gather x1, waiting for transfers between devices, on_device(): lax.all_gather(out_weight, ('far', 'near'), axis=0, tiled=False)  8.08 us
    pallas_call x1, Pallas kernels, on_device(): pl.pallas_call(functools.partial(project, share), grid=(members,), out_sh...  7.12 us
  transfers between devices with their start and end apart: 4, of which 3 were waited for; matrix products, arithmetic and copies ran while one was open for 0% of the time, Pallas kernels for 1%

profile of v3, /device:TPU:65, one launch (start us, length us, event | category | flops | bytes accessed | tf_op | source)
XLA Modules:
  0.0 180.4 jit_solution(12555470597272212240)
XLA Ops:
  6.5 0.0 all-gather.5.cloned.1.call-start
  6.6 0.7 all-gather.5.cloned.1.call-update
  7.4 0.3 fusion
  7.7 0.0 copy-start.1
  7.7 0.9 copy-done.1
  8.7 0.0 copy-start.2
  8.7 0.8 copy-done.2
  9.4 0.0 copy-start.3
  9.4 0.8 copy-done.3
  10.2 0.2 prepare.1
  10.4 48.4 %all-gather = bf16[8,128,128]{2,1,0:T(8,128)(2,1)S(1)} all-gather(bf16[2,128,128]{2,1,0:T(8,128)(2,1)S(1)} %get-tuple-element.10), channel_id=2, replica_groups=mesh['groups'=2,'far'=4,'near'=4,'core'=2,'tp'=8] {'far'}, dimensions={0}, use_global_device_ids=true | all-gather | bytes 327680 | tf_op jit(solution)/shard_map/all_gather | solution.py:149
  58.8 32.6 %all-gather.1 = bf16[12,2,128,128]{3,2,1,0:T(8,128)(2,1)S(1)} all-gather(bf16[3,2,128,128]{3,2,1,0:T(8,128)(2,1)S(1)} %pad_maximum_fusion), channel_id=3, replica_groups=mesh['groups'=2,'far'=4,'near'=4,'core'=2,'tp'=8] {'near'}, dimensions={0}, use_global_device_ids=true | all-gather | bytes 983040 | tf_op jit(solution)/shard_map/all_gather | solution.py:157
  91.4 8.9 %collective-permute-start = (bf16[4,3,2,128,128]{4,3,2,1,0:T(8,128)(2,1)S(1)}, bf16[4,3,2,128,128]{4,3,2,1,0:T(8,128)(2,1)S(1)}, u32[]{:S(2)}, u32[]{:S(2)}) collective-permute-start(bf16[4,3,2,128,128]{4,3,2,1,0:T(8,128)(2,1)S(1)} %bitcast.8), channel_id=1, source_target_pairs={{0,8},{8,0},{1,9},{9,1},{2,10},{10,2},{3,11},{11,3},{4,12},{12,4},... | collective-permute-start | bytes 2359304 | tf_op jit(solution)/shard_map/ppermute | solution.py:158
  100.3 1.9 %collective-permute-done.b_ref = bf16[4,3,2,128,128]{4,3,2,1,0:T(8,128)(2,1)S(1)} collective-permute-done((bf16[4,3,2,128,128]{4,3,2,1,0:T(8,128)(2,1)S(1)}, bf16[4,3,2,128,128]{4,3,2,1,0:T(8,128)(2,1)S(1)}, u32[]{:S(2)}, u32[]{:S(2)}) %collective-permute-start) | collective-permute-done | bytes 786464 | tf_op jit(solution)/shard_map/ppermute | solution.py:158
  102.2 0.0 copy-start.4
  102.2 0.7 copy-done.4
  102.9 1.3 attend.1.own_ref
  104.2 0.0 copy-start
  104.2 2.3 %collective-permute-start.1 = (bf16[128,1024]{1,0:T(8,128)(2,1)S(1)}, bf16[128,1024]{1,0:T(8,128)(2,1)S(1)}, u32[]{:S(2)}, u32[]{:S(2)}) collective-permute-start(bf16[128,1024]{1,0:T(8,128)(2,1)S(1)} %attend.1.own_ref), channel_id=1, source_target_pairs={{0,8},{8,0},{1,9},{9,1},{2,10},{10,2},{3,11},{11,3},{4,12},{12,4},... | collective-permute-start | bytes 786440 | tf_op jit(solution)/shard_map/ppermute | solution.py:182
  106.6 11.7 %all_to_all.10.level_ref = bf16[8,8,128]{2,1,0:T(8,128)(2,1)} all-to-all(bf16[8,8,128]{2,1,0:T(8,128)(2,1)S(1)} %slice_bitcast_fusion), channel_id=1, replica_groups=mesh['groups'=2,'far'=4,'near'=4,'core'=2,'tp'=8] {'tp'}, dimensions={0} | all-to-all | bytes 32768 | tf_op jit(solution)/shard_map/all_to_all | solution.py:175
  118.3 0.0 collective-permute-done.1.other_ref
  118.3 0.0 copy-start.5
  118.3 8.1 %all-gather.5.cloned.1.call-done = bf16[16384,128]{1,0:T(8,128)(2,1)} async-done(((bf16[1024,128]{1,0:T(8,128)(2,1)}), bf16[16384,128]{1,0:T(8,128)(2,1)}) %all-gather.5.cloned.1.call-update) | async-done | bytes 4194320 | tf_op jit(solution)/shard_map/all_gather | solution.py:132
  126.4 0.0 copy-done
  126.4 0.0 copy-done.5
  126.4 7.1 %project.1 = bf16[8,256,256]{2,1,0:T(8,128)(2,1)} custom-call(bf16[8,8,128]{2,1,0:T(8,128)(2,1)} %all_to_all.10.level_ref, bf16[128,1024]{1,0:T(8,128)(2,1)} %copy-done, bf16[128,1024]{1,0:T(8,128)(2,1)} %copy-done.5, bf16[16,1024,128]{2,1,0:T(8,128)(2,1)} %bitcast.11, bf16[16,1024,128]{2,1,0:T(8,128)(2,1)} %bitcast.12), custom_call_target="tpu_custom_call" | custom-call | flops 1000000000 | bytes 10000000 | tf_op jit(solution)/shard_map/project/pallas_call | solution.py:186
  133.5 27.1 %all_to_all.11.terms_ref = bf16[8,256,256]{2,1,0:T(8,128)(2,1)S(1)} all-to-all(bf16[8,256,256]{2,1,0:T(8,128)(2,1)} %project.1), channel_id=1, replica_groups=mesh['groups'=2,'far'=4,'near'=4,'core'=2,'tp'=8] {'tp'}, dimensions={0} | all-to-all | bytes 2097152 | tf_op jit(solution)/shard_map/all_to_all | solution.py:199
  160.6 0.1 total.1
  160.7 11.2 %collective-permute-start.2 = (bf16[128,256]{1,0:T(8,128)(2,1)S(1)}, bf16[128,256]{1,0:T(8,128)(2,1)S(1)}, u32[]{:S(2)}, u32[]{:S(2)}) collective-permute-start(bf16[128,256]{1,0:T(8,128)(2,1)S(1)} %get-tuple-element.12), channel_id=1, source_target_pairs={{0,8},{8,0},{1,9},{9,1},{2,10},{10,2},{3,11},{11,3},{4,12},{12,4},... | collective-permute-start | bytes 196616 | tf_op jit(solution)/shard_map/ppermute | solution.py:209
  172.0 0.9 collective-permute-done.2.given_ref
  172.9 0.7 weave.1
  (5 shorter events, 0.1 us)
Async XLA Ops:
  6.5 119.8 %all-gather.5.cloned.1.call-start = ((), (), s32[]{:S(2)}) async-start(), calls=%async_computation.2 | async-start | bytes 4456448 | tf_op jit(solution)/shard_map/all_gather | solution.py:132
  7.7 1.0 copy-start.1
  8.7 0.8 copy-start.2
  9.4 0.8 copy-start.3
  91.4 10.8 %collective-permute-start = (bf16[4,3,2,128,128]{4,3,2,1,0:T(8,128)(2,1)S(1)}, bf16[4,3,2,128,128]{4,3,2,1,0:T(8,128)(2,1)S(1)}, u32[]{:S(2)}, u32[]{:S(2)}) collective-permute-start(bf16[4,3,2,128,128]{4,3,2,1,0:T(8,128)(2,1)S(1)} %bitcast.8), channel_id=1, source_target_pairs={{0,8},{8,0},{1,9},{9,1},{2,10},{10,2},{3,11},{11,3},{4,12},{12,4},... | collective-permute-start | bytes 2359304 | tf_op jit(solution)/shard_map/ppermute | solution.py:158
  102.2 0.7 copy-start.4
  104.2 22.1 %copy-start = (bf16[128,1024]{1,0:T(8,128)(2,1)}, bf16[128,1024]{1,0:T(8,128)(2,1)S(1)}, u32[]{:S(2)}) copy-start(bf16[128,1024]{1,0:T(8,128)(2,1)S(1)} %attend.1.own_ref) | copy-start | bytes 786436
  104.2 14.0 %collective-permute-start.1 = (bf16[128,1024]{1,0:T(8,128)(2,1)S(1)}, bf16[128,1024]{1,0:T(8,128)(2,1)S(1)}, u32[]{:S(2)}, u32[]{:S(2)}) collective-permute-start(bf16[128,1024]{1,0:T(8,128)(2,1)S(1)} %attend.1.own_ref), channel_id=1, source_target_pairs={{0,8},{8,0},{1,9},{9,1},{2,10},{10,2},{3,11},{11,3},{4,12},{12,4},... | collective-permute-start | bytes 786440 | tf_op jit(solution)/shard_map/ppermute | solution.py:182
  118.3 8.1 %copy-start.5 = (bf16[128,1024]{1,0:T(8,128)(2,1)}, bf16[128,1024]{1,0:T(8,128)(2,1)S(1)}, u32[]{:S(2)}) copy-start(bf16[128,1024]{1,0:T(8,128)(2,1)S(1)} %collective-permute-done.1.other_ref) | copy-start | bytes 786436
  160.7 12.1 %collective-permute-start.2 = (bf16[128,256]{1,0:T(8,128)(2,1)S(1)}, bf16[128,256]{1,0:T(8,128)(2,1)S(1)}, u32[]{:S(2)}, u32[]{:S(2)}) collective-permute-start(bf16[128,256]{1,0:T(8,128)(2,1)S(1)} %get-tuple-element.12), channel_id=1, source_target_pairs={{0,8},{8,0},{1,9},{9,1},{2,10},{10,2},{3,11},{11,3},{4,12},{12,4},... | collective-permute-start | bytes 196616 | tf_op jit(solution)/shard_map/ppermute | solution.py:209
Sparse Core Ops, SparseCore 0:
  9.4 116.8 all-gather.4

commit v4 on v3

--- a/solution.py
+++ b/solution.py
@@ -94,31 +94,13 @@
         )
 
 
-def project(count, level_ref, own_ref, other_ref, *refs):
+def project(count, parts, level_ref, a_ref, *refs):
     out_ref = refs[count]
-    rows = own_ref.shape[0]
+    width = out_ref.shape[2]
     weights = jnp.concatenate([w_ref[0] for w_ref in refs[:count]], 1)
-    for i, a_ref in enumerate((own_ref, other_ref)):
-        out_ref[0, i * rows : (i + 1) * rows] = jnp.dot(
-            a_ref[...], weights, preferred_element_type=jnp.float32
-        ).astype(jnp.bfloat16)
-
-
-def total(terms_ref, kept_ref, sent_ref):
-    rows = kept_ref.shape[0]
-    for i, out_ref in enumerate((kept_ref, sent_ref)):
-        at = slice(i * rows, (i + 1) * rows)
-        out_ref[...] = jnp.sum(terms_ref[:, at].astype(jnp.float32), 0).astype(jnp.bfloat16)
-
-
-def weave(count, core, kept_ref, given_ref, out_ref):
-    width = kept_ref.shape[1] // count
-    even = core[0] == 0
-    for j in range(count):
-        kept, given = (r[:, j * width : (j + 1) * width] for r in (kept_ref, given_ref))
-        at = j * CORES * width
-        out_ref[:, at : at + width] = jnp.where(even, kept, given)
-        out_ref[:, at + width : at + CORES * width] = jnp.where(even, given, kept)
+    terms = jnp.dot(a_ref[...], weights, preferred_element_type=jnp.float32).astype(jnp.bfloat16)
+    for i in range(parts):
+        out_ref[i] = terms[:, i * width : (i + 1) * width]
 
 
 def on_device(query_matrix, key_matrix, value_matrix, doc_ids, out_weight):
@@ -129,7 +111,7 @@
     core = lax.axis_index("core")
     my_line = lax.axis_index("far")
     ctx_index = (my_line * line + lax.axis_index("near")) * CORES + core
-    weight_blocks = lax.all_gather(out_weight, ("far", "near"), axis=0, tiled=False)
+    weight_blocks = lax.all_gather(out_weight, ("far", "near", "core"), axis=0, tiled=False)
     given_pos = ctx_index * tok_rows + jnp.arange(tok_rows, dtype=jnp.int32)
     vmem = pl.BlockSpec(memory_space=pltpu.VMEM)
     small = pltpu.CompilerParams(vmem_limit_bytes=16 * 2**20)
@@ -179,42 +161,25 @@
         concat_axis=0,
         tiled=True,
     )
-    attention_other = lax.ppermute(attention, "core", swap)
     blocks, depth, width = weight_blocks.shape
     share = blocks // members
-    whole = pl.BlockSpec((tok_rows, depth), lambda i: (0, 0))
+    parts = math.gcd(members, 2)
+    count = share * parts
     terms = pl.pallas_call(
-        functools.partial(project, share),
-        grid=(members,),
-        out_shape=jax.ShapeDtypeStruct((members, CORES * tok_rows, share * width), jnp.bfloat16),
-        in_specs=[pl.BlockSpec(memory_space=pl.ANY), whole, whole]
+        functools.partial(project, count, parts),
+        grid=(blocks // count,),
+        out_shape=jax.ShapeDtypeStruct((members, tok_rows, share * width), jnp.bfloat16),
+        in_specs=[pl.BlockSpec(memory_space=pl.ANY), pl.BlockSpec((tok_rows, depth), lambda i: (0, 0))]
         + [
-            pl.BlockSpec((1, depth, width), lambda i, j=j: (i * share + j, 0, 0))
-            for j in range(share)
+            pl.BlockSpec((1, depth, width), lambda i, j=j: (i * count + j, 0, 0))
+            for j in range(count)
         ],
-        out_specs=pl.BlockSpec((1, CORES * tok_rows, share * width), lambda i: (i, 0, 0)),
+        out_specs=pl.BlockSpec((parts, tok_rows, share * width), lambda i: (i, 0, 0)),
         cost_estimate=pl.CostEstimate(flops=10**9, bytes_accessed=10**7, transcendentals=0),
         name="project",
-    )(level, attention, attention_other, *[weight_blocks] * share)
+    )(level, attention, *[weight_blocks] * count)
     arrived = lax.all_to_all(terms, "tp", split_axis=0, concat_axis=0, tiled=True)
-    half = jax.ShapeDtypeStruct((tok_rows, share * width), jnp.bfloat16)
-    kept, sent = pl.pallas_call(
-        total,
-        out_shape=(half, half),
-        in_specs=[vmem],
-        out_specs=(vmem, vmem),
-        compiler_params=small,
-        name="total",
-    )(arrived)
-    given = lax.ppermute(sent, "core", swap)
-    return pl.pallas_call(
-        functools.partial(weave, share),
-        out_shape=jax.ShapeDtypeStruct((tok_rows, share * CORES * width), jnp.bfloat16),
-        in_specs=[pl.BlockSpec(memory_space=pltpu.SMEM), vmem, vmem],
-        out_specs=vmem,
-        compiler_params=small,
-        name="weave",
-    )(core.astype(jnp.int32).reshape(1), kept, given)
+    return arrived.astype(jnp.float32).sum(axis=0).astype(jnp.bfloat16)
 
 
 def solution(mesh):

time: 181 us -> 184 us (1.017)
  starting transfers between devices: 22.4 us -> 9.1 us
  blocking collectives: 120 us -> 129 us
  waiting for transfers between devices: 11.6 us -> 20 us
  Pallas kernels: 9.44 us -> 7.47 us
    ppermute x2 -> x0, starting transfers between devices: 13.6 us -> none  [the longest x1 11.2 us: on_device(): given = lax.ppermute(sent, 'core', swap)]
    all_gather x1, waiting for transfers between devices: 8.08 us -> 17.3 us  [on_device(): lax.all_gather(out_weight, ('far', 'near', 'core'), axis=0, tiled=False)]
    all_to_all x1, blocking collectives: 27.1 us -> 36 us  [on_device(): lax.all_to_all(terms, 'tp', split_axis=0, concat_axis=0, tiled=True)]
    pallas_call x3 -> x1, Pallas kernels: 7.93 us -> 5.96 us  [on_device(): pl.pallas_call(functools.partial(project, count, parts), grid=(blocks //...]
  transfers between devices with their start and end apart: 4 -> 2, of which waited for: 3 -> 2; matrix products, arithmetic and copies ran while one was open for 0% -> 0% of each run, Pallas kernels for 1% -> 1%
where the time goes in v4:
time: 184 us; the launch traced here: 183 us
  blocking collectives  129 us (70%)
  waiting for transfers between devices  20 us (11%)
  between operations  13.6 us (7%)
  starting transfers between devices  9.1 us (5%)
  Pallas kernels  7.47 us (4%)
  local copies, waits for them, and re-layouts  3.2 us (2%)
    all_gather x1, blocking collectives, on_device(): far = lax.all_gather(here, 'far', axis=0, tiled=False)  48.4 us
    all_to_all x1, blocking collectives, on_device(): lax.all_to_all(terms, 'tp', split_axis=0, concat_axis=0, tiled=True)  36 us
    all_gather x1, blocking collectives, on_device(): mine = lax.all_gather(wanted, 'near', axis=0, tiled=False)  32.4 us
    all_gather x1, waiting for transfers between devices, on_device(): lax.all_gather(out_weight, ('far', 'near', 'core'), axis=0, tiled=False)  17.3 us
    all_to_all x1, blocking collectives, on_device(): lax.all_to_all(attention[:members * 8, :HEAD_SIZE].reshape(members, 8, HE...  11.8 us
    ppermute x1, starting transfers between devices, on_device(): theirs = lax.ppermute(mine, 'core', swap)  9.09 us
    pallas_call x1, Pallas kernels, on_device(): pl.pallas_call(functools.partial(project, count, parts), grid=(blocks //...  5.96 us
  transfers between devices with their start and end apart: 2, of which 2 were waited for; matrix products, arithmetic and copies ran while one was open for 0% of the time, Pallas kernels for 1%

profile of v4, /device:TPU:65, one launch (start us, length us, event | category | flops | bytes accessed | tf_op | source)
XLA Modules:
  0.0 183.1 jit_solution(2086307945850123781)
XLA Ops:
  6.5 0.0 all-gather.5.cloned.1.call-start
  6.6 0.7 all-gather.5.cloned.1.call-update
  7.4 0.3 fusion
  7.7 0.0 copy-start.1
  7.7 0.9 copy-done.1
  8.7 0.0 copy-start.2
  8.7 0.8 copy-done.2
  9.4 0.0 copy-start.3
  9.4 0.8 copy-done.3
  10.2 0.2 prepare.1
  10.4 48.4 %all-gather = bf16[8,128,128]{2,1,0:T(8,128)(2,1)S(1)} all-gather(bf16[2,128,128]{2,1,0:T(8,128)(2,1)S(1)} %get-tuple-element.8), channel_id=2, replica_groups=mesh['groups'=2,'far'=4,'near'=4,'core'=2,'tp'=8] {'far'}, dimensions={0}, use_global_device_ids=true | all-gather | bytes 327680 | tf_op jit(solution)/shard_map/all_gather | solution.py:131
  58.8 32.4 %all-gather.1 = bf16[12,2,128,128]{3,2,1,0:T(8,128)(2,1)S(1)} all-gather(bf16[3,2,128,128]{3,2,1,0:T(8,128)(2,1)S(1)} %pad_maximum_fusion), channel_id=3, replica_groups=mesh['groups'=2,'far'=4,'near'=4,'core'=2,'tp'=8] {'near'}, dimensions={0}, use_global_device_ids=true | all-gather | bytes 983040 | tf_op jit(solution)/shard_map/all_gather | solution.py:139
  91.2 9.1 %collective-permute-start = (bf16[4,3,2,128,128]{4,3,2,1,0:T(8,128)(2,1)S(1)}, bf16[4,3,2,128,128]{4,3,2,1,0:T(8,128)(2,1)S(1)}, u32[]{:S(2)}, u32[]{:S(2)}) collective-permute-start(bf16[4,3,2,128,128]{4,3,2,1,0:T(8,128)(2,1)S(1)} %bitcast.7), channel_id=1, source_target_pairs={{0,8},{8,0},{1,9},{9,1},{2,10},{10,2},{3,11},{11,3},{4,12},{12,4},... | collective-permute-start | bytes 2359304 | tf_op jit(solution)/shard_map/ppermute | solution.py:140
  100.3 2.0 %collective-permute-done.b_ref = bf16[4,3,2,128,128]{4,3,2,1,0:T(8,128)(2,1)S(1)} collective-permute-done((bf16[4,3,2,128,128]{4,3,2,1,0:T(8,128)(2,1)S(1)}, bf16[4,3,2,128,128]{4,3,2,1,0:T(8,128)(2,1)S(1)}, u32[]{:S(2)}, u32[]{:S(2)}) %collective-permute-start) | collective-permute-done | bytes 786464 | tf_op jit(solution)/shard_map/ppermute | solution.py:140
  102.3 0.0 copy-start.4
  102.3 0.7 copy-done.4
  103.0 1.3 attend.1.a_ref
  104.3 0.0 copy-start
  104.3 11.8 %all_to_all.10.level_ref = bf16[8,8,128]{2,1,0:T(8,128)(2,1)} all-to-all(bf16[8,8,128]{2,1,0:T(8,128)(2,1)S(1)} %slice_bitcast_fusion), channel_id=1, replica_groups=mesh['groups'=2,'far'=4,'near'=4,'core'=2,'tp'=8] {'tp'}, dimensions={0} | all-to-all | bytes 32768 | tf_op jit(solution)/shard_map/all_to_all | solution.py:157
  116.2 17.3 %all-gather.5.cloned.1.call-done = bf16[32768,128]{1,0:T(8,128)(2,1)} async-done(((bf16[1024,128]{1,0:T(8,128)(2,1)}), bf16[32768,128]{1,0:T(8,128)(2,1)}) %all-gather.5.cloned.1.call-update) | async-done | bytes 8388624 | tf_op jit(solution)/shard_map/all_gather | solution.py:114
  133.4 0.0 copy-done
  133.4 6.0 %project.1 = bf16[8,128,512]{2,1,0:T(8,128)(2,1)} custom-call(bf16[8,8,128]{2,1,0:T(8,128)(2,1)} %all_to_all.10.level_ref, bf16[128,1024]{1,0:T(8,128)(2,1)} %copy-done, bf16[32,1024,128]{2,1,0:T(8,128)(2,1)} %bitcast.10, bf16[32,1024,128]{2,1,0:T(8,128)(2,1)} %bitcast.11, bf16[32,1024,128]{2,1,0:T(8,128)(2,1)} %bitcast.12, bf16[32,1024,128]{2,1,0:T(8,128)(2,1)} %bitcast.13, ...), custom_call_target="tpu_custom_call" | custom-call | flops 1000000000 | bytes 10000000 | tf_op jit(solution)/shard_map/project/pallas_call | solution.py:168
  139.4 36.0 %all_to_all.11 = bf16[8,128,512]{2,1,0:T(8,128)(2,1)S(1)} all-to-all(bf16[8,128,512]{2,1,0:T(8,128)(2,1)} %project.1), channel_id=1, replica_groups=mesh['groups'=2,'far'=4,'near'=4,'core'=2,'tp'=8] {'tp'}, dimensions={0} | all-to-all | bytes 2097152 | tf_op jit(solution)/shard_map/all_to_all | solution.py:181
  175.4 0.8 reduce_sum.12
  (5 shorter events, 0.1 us)
Async XLA Ops:
  6.5 126.9 %all-gather.5.cloned.1.call-start = ((), (), s32[]{:S(2)}) async-start(), calls=%async_computation.2 | async-start | bytes 8650752 | tf_op jit(solution)/shard_map/all_gather | solution.py:114
  7.7 1.0 copy-start.1
  8.7 0.8 copy-start.2
  9.4 0.8 copy-start.3
  91.2 11.1 %collective-permute-start = (bf16[4,3,2,128,128]{4,3,2,1,0:T(8,128)(2,1)S(1)}, bf16[4,3,2,128,128]{4,3,2,1,0:T(8,128)(2,1)S(1)}, u32[]{:S(2)}, u32[]{:S(2)}) collective-permute-start(bf16[4,3,2,128,128]{4,3,2,1,0:T(8,128)(2,1)S(1)} %bitcast.7), channel_id=1, source_target_pairs={{0,8},{8,0},{1,9},{9,1},{2,10},{10,2},{3,11},{11,3},{4,12},{12,4},... | collective-permute-start | bytes 2359304 | tf_op jit(solution)/shard_map/ppermute | solution.py:140
  102.3 0.7 copy-start.4
  104.3 29.1 %copy-start = (bf16[128,1024]{1,0:T(8,128)(2,1)}, bf16[128,1024]{1,0:T(8,128)(2,1)S(1)}, u32[]{:S(2)}) copy-start(bf16[128,1024]{1,0:T(8,128)(2,1)S(1)} %attend.1.a_ref) | copy-start | bytes 786436
Sparse Core Ops, SparseCore 0:
  9.5 123.9 all-gather.4

commit v5 on v2

v5 whole, which is shorter than its diff:
```python
import functools
import math

import jax
import jax.numpy as jnp
from jax import lax
from jax.experimental import pallas as pl
from jax.experimental.pallas import tpu as pltpu
from jax.sharding import Mesh
from jax.sharding import PartitionSpec as P

HEAD_SIZE = 128
CORES = 2
DOCS = 6


rope_base = 1000000.0


def rotary_tables(token_positions):
    half_dim = HEAD_SIZE // 2
    lane = jnp.arange(HEAD_SIZE, dtype=jnp.int32)
    power = -(lane % half_dim).astype(jnp.float32) * (2.0 / HEAD_SIZE)
    angles = token_positions.astype(jnp.float32)[:, None] * jnp.power(jnp.float32(rope_base), power)
    return jnp.cos(angles), jnp.where(lane < half_dim, -1.0, 1.0) * jnp.sin(angles)


def prepare(heads, info, cosine_ref, sine_ref, q_hbm, k_hbm, v_hbm, doc_hbm, q_out, k_out, v_out, first_out, q_ref, k_ref, v_ref, doc_ref, sems):
    pairs = ((k_hbm, k_ref), (v_hbm, v_ref), (q_hbm, q_ref), (doc_hbm, doc_ref))
    copies = [pltpu.make_async_copy(a, b, sems.at[i]) for i, (a, b) in enumerate(pairs)]
    for copy in copies:
        copy.start()
    cosine, sine = cosine_ref[...], sine_ref[...]

    def turned(x):
        x = x.astype(jnp.float32)
        return (x * cosine + pltpu.roll(x, HEAD_SIZE // 2, 1) * sine).astype(jnp.bfloat16)

    copies[0].wait()
    k_out[...] = turned(k_ref[...])
    copies[1].wait()
    v_out[...] = v_ref[...].astype(jnp.float32).T.astype(jnp.bfloat16)
    copies[2].wait()
    for h in range(heads):
        q_out[h] = turned(q_ref[:, h * HEAD_SIZE : (h + 1) * HEAD_SIZE])
    copies[3].wait()
    docs, here = doc_ref[...], doc_ref[pl.ds(info[0], 1), :]
    first = jnp.zeros(here.shape, jnp.int32)
    for d in range(1, DOCS):
        before = jnp.sum((docs < d).astype(jnp.int32), keepdims=True)
        first = first + jnp.where(here == d, before, 0)
    first_out[...] = jnp.broadcast_to(first, first_out.shape)


def attend(heads, together, info, first_ref, q_ref, ka_ref, kb_ref, va_ref, vb_ref, out_ref, m_ref, l_ref, acc_ref):
    rows = ka_ref.shape[1]
    ctx = info[0]
    core = lax.rem(ctx, CORES)
    chip = lax.div(ctx, CORES)
    scale = HEAD_SIZE**-0.5 * math.log2(math.e)
    m_ref[...] = jnp.full(m_ref.shape, -1e30, jnp.float32)
    l_ref[...] = jnp.zeros(l_ref.shape, jnp.float32)
    acc_ref[...] = jnp.zeros(acc_ref.shape, jnp.float32)
    width = CORES * rows
    key = lax.broadcasted_iota(jnp.int32, (width, rows), 0)
    given = ctx * rows + lax.broadcasted_iota(jnp.int32, (width, rows), 1)
    mine = key < rows
    first = first_ref[0:1, :]
    first_chip = lax.div(jnp.min(first), width)

    def one_chip(step, carry):
        at = chip - step
        own = (at * CORES + core) * rows
        other = (at * CORES + (1 - core)) * rows - rows
        position = key + jnp.where(mine, own, other)
        bias = jnp.where((position >= first) & (position <= given), 0.0, -1e30)
        bias = jnp.concatenate([bias] * together, 1)
        keys = jnp.concatenate([ka_ref[at], kb_ref[at]], 0)
        values = jnp.concatenate([va_ref[at], vb_ref[at]], 1)
        for g in range(heads // together):
            q = q_ref[g * together : (g + 1) * together].reshape(together * rows, HEAD_SIZE)
            scores = lax.dot_general(
                keys, q, (((1,), (1,)), ((), ())), preferred_element_type=jnp.float32
            )
            scores = scores + bias
            old = m_ref[g]
            new = jnp.maximum(old, jnp.max(scores, 0, keepdims=True))
            weights = jnp.exp2((scores - new) * scale)
            factor = jnp.exp2((old - new) * scale)
            m_ref[g] = new
            l_ref[g] = l_ref[g] * factor + jnp.sum(weights, 0, keepdims=True)
            acc_ref[g] = acc_ref[g] * factor + jnp.dot(
                values, weights.astype(jnp.bfloat16), preferred_element_type=jnp.float32
            )
        return carry

    lax.fori_loop(0, chip - first_chip + 1, one_chip, 0)
    for g in range(heads // together):
        mixed = acc_ref[g] / l_ref[g]
        for i in range(together):
            h = g * together + i
            out_ref[:, h * HEAD_SIZE : (h + 1) * HEAD_SIZE] = mixed[
                :, i * rows : (i + 1) * rows
            ].T.astype(jnp.bfloat16)


def project(count, parts, a_ref, *refs):
    out_ref = refs[count]
    width = out_ref.shape[2]
    weights = jnp.concatenate([w_ref[0] for w_ref in refs[:count]], 1)
    terms = jnp.dot(a_ref[...], weights, preferred_element_type=jnp.float32).astype(jnp.bfloat16)
    for i in range(parts):
        out_ref[i] = terms[:, i * width : (i + 1) * width]


def on_device(query_matrix, key_matrix, value_matrix, doc_ids, out_weight):
    tok_rows = query_matrix.shape[0]
    query_heads = query_matrix.shape[1] // HEAD_SIZE
    members = lax.axis_size("tp")
    ctx_index = lax.axis_index("z") * CORES + lax.axis_index("core")
    weight_blocks = lax.all_gather(out_weight, ("z", "core"), axis=0, tiled=False)
    given_pos = ctx_index * tok_rows + jnp.arange(tok_rows, dtype=jnp.int32)
    info = ctx_index.astype(jnp.int32).reshape(1)
    docs = doc_ids.reshape(-1, tok_rows)
    vmem = pl.BlockSpec(memory_space=pltpu.VMEM)
    smem = pl.BlockSpec(memory_space=pltpu.SMEM)
    hbm = pl.BlockSpec(memory_space=pltpu.HBM)
    small = pltpu.CompilerParams(vmem_limit_bytes=16 * 2**20)
    queries, keys_here, values_here, first = pl.pallas_call(
        functools.partial(prepare, query_heads),
        out_shape=(
            jax.ShapeDtypeStruct((query_heads, tok_rows, HEAD_SIZE), jnp.bfloat16),
            jax.ShapeDtypeStruct(key_matrix.shape, jnp.bfloat16),
            jax.ShapeDtypeStruct(value_matrix.shape[::-1], jnp.bfloat16),
            jax.ShapeDtypeStruct((8, tok_rows), jnp.int32),
        ),
        in_specs=[smem, vmem, vmem] + [hbm] * 4,
        out_specs=(vmem,) * 4,
        scratch_shapes=[
            pltpu.VMEM(x.shape, x.dtype) for x in (query_matrix, key_matrix, value_matrix, docs)
        ]
        + [pltpu.SemaphoreType.DMA((4,))],
        cost_estimate=pl.CostEstimate(flops=10**6, bytes_accessed=10**6, transcendentals=0),
        name="prepare",
    )(info, *rotary_tables(given_pos), query_matrix, key_matrix, value_matrix, docs)
    swap = [(i, CORES - 1 - i) for i in range(CORES)]
    keys_a = lax.all_gather(keys_here, "z", axis=0, tiled=False)
    keys_b = lax.ppermute(keys_a, "core", swap)
    values_a = lax.all_gather(values_here, "z", axis=0, tiled=False)
    values_b = lax.ppermute(values_a, "core", swap)
    together = math.gcd(query_heads, 2)
    sets = query_heads // together
    attention = pl.pallas_call(
        functools.partial(attend, query_heads, together),
        out_shape=jax.ShapeDtypeStruct((tok_rows, query_heads * HEAD_SIZE), jnp.bfloat16),
        in_specs=[smem] + [vmem] * 6,
        out_specs=vmem,
        scratch_shapes=[
            pltpu.VMEM((sets, 1, together * tok_rows), jnp.float32),
            pltpu.VMEM((sets, 1, together * tok_rows), jnp.float32),
            pltpu.VMEM((sets, HEAD_SIZE, together * tok_rows), jnp.float32),
        ],
        cost_estimate=pl.CostEstimate(flops=2 * 10**9, bytes_accessed=3 * 10**6, transcendentals=10**6),
        compiler_params=small,
        name="attend",
    )(info, first, queries, keys_a, keys_b, values_a, values_b)
    blocks, depth, width = weight_blocks.shape
    share = blocks // members
    parts = math.gcd(members, 2)
    count = share * parts
    terms = pl.pallas_call(
        functools.partial(project, count, parts),
        grid=(blocks // count,),
        out_shape=jax.ShapeDtypeStruct((members, tok_rows, share * width), jnp.bfloat16),
        in_specs=[pl.BlockSpec((tok_rows, depth), lambda i: (0, 0))]
        + [
            pl.BlockSpec((1, depth, width), lambda i, j=j: (i * count + j, 0, 0))
            for j in range(count)
        ],
        out_specs=pl.BlockSpec((parts, tok_rows, share * width), lambda i: (i, 0, 0)),
        cost_estimate=pl.CostEstimate(flops=10**9, bytes_accessed=10**7, transcendentals=0),
        name="project",
    )(attention, *[weight_blocks] * count)
    arrived = lax.all_to_all(terms, "tp", split_axis=0, concat_axis=0, tiled=True)
    return arrived.astype(jnp.float32).sum(axis=0).astype(jnp.bfloat16)


def solution(mesh):
    groups, ctx, tp = mesh.devices.shape
    fine = Mesh(mesh.devices.reshape(groups, ctx // CORES, CORES, tp), ("groups", "z", "core", "tp"))
    tokens = ("groups", "z", "core")
    in_specs = (P(tokens, "tp"), P(tokens, "tp"), P(tokens, "tp"), P("groups"), P("tp", ("z", "core")))
    return jax.shard_map(
        on_device, mesh=fine, in_specs=in_specs, out_specs=P(tokens, "tp"), check_vma=False
    )
```

time: 180 us -> 178 us (0.989)
  waiting for transfers between devices: 4.63 us -> 2.26 us
  starting transfers between devices: 14.1 us -> 16.3 us
  blocking collectives: 133 us -> 131 us
    pallas_call x1, Pallas kernels: 0.2 us -> 2.78 us  [on_device(): pl.pallas_call(functools.partial(prepare, query_heads), out_shape=(jax.Sh...]
    all_gather x1, waiting for transfers between devices: 2.37 us -> 0.01 us  [on_device(): lax.all_gather(out_weight, ('z', 'core'), axis=0, tiled=False)]
    ppermute x1, starting transfers between devices: 7.79 us -> 9.78 us  [on_device(): keys_b = lax.ppermute(keys_a, 'core', swap)]
    unnamed x10 -> x6, local copies, waits for them, and re-layouts: 3.87 us -> 2.31 us
  transfers between devices with their start and end apart: 3 -> 3, of which waited for: 2 -> 1; matrix products, arithmetic and copies ran while one was open for 0% -> 1% of each run, Pallas kernels for 1% -> 2%
where the time goes in v5:
time: 178 us; the launch traced here: 177 us
  blocking collectives  131 us (74%)
  starting transfers between devices  16.3 us (9%)
  between operations  13.5 us (8%)
  Pallas kernels  10.3 us (6%)
  local copies, waits for them, and re-layouts  2.31 us (1%)
  waiting for transfers between devices  2.26 us (1%)
  other arithmetic  1.79 us (1%)
    all_gather x1, blocking collectives, on_device(): keys_a = lax.all_gather(keys_here, 'z', axis=0, tiled=False)  67.9 us
    all_to_all x1, blocking collectives, on_device(): lax.all_to_all(terms, 'tp', split_axis=0, concat_axis=0, tiled=True)  34.1 us
    all_gather x1, blocking collectives, on_device(): values_a = lax.all_gather(values_here, 'z', axis=0, tiled=False)  28.8 us
    ppermute x1, starting transfers between devices, on_device(): keys_b = lax.ppermute(keys_a, 'core', swap)  9.78 us
    ppermute x1, starting transfers between devices, on_device(): values_b = lax.ppermute(values_a, 'core', swap)  6.49 us
    pallas_call x1, Pallas kernels, on_device(): pl.pallas_call(functools.partial(project, count, parts), grid=(blocks //...  5.95 us
  transfers between devices with their start and end apart: 3, of which 1 were waited for; matrix products, arithmetic and copies ran while one was open for 1% of the time, Pallas kernels for 2%

profile of v5, /device:TPU:65, one launch (start us, length us, event | category | flops | bytes accessed | tf_op | source)
XLA Modules:
  0.0 177.2 jit_solution(443258724529601850)
XLA Ops:
  6.5 0.0 all-gather.5.cloned.1.call-start
  6.6 0.7 all-gather.5.cloned.1.call-update
  7.3 1.0 fusion
  8.3 2.8 %prepare.1 = (bf16[8,128,128]{2,1,0:T(8,128)(2,1)}, bf16[128,128]{1,0:T(8,128)(2,1)}, bf16[128,128]{1,0:T(8,128)(2,1)}, s32[8,128]{1,0:T(8,128)}) custom-call(s32[1]{0:T(128)} %bitcast.info, f32[128,128]{1,0:T(8,128)} %get-tuple-element.14.cosine_ref, f32[128,128]{1,0:T(8,128)} %get-tuple-element.13.sine_ref, bf16[128,1024]{1,0:T(8,128)(2,1)} %q_hbm.1, ...), custom_call_target="tpu_custom_call" | custom-call | flops 1000000 | bytes 1000000 | tf_op jit(solution)/shard_map/prepare/pallas_call | solution.py:129
  11.1 67.9 %all-gather = bf16[2048,128]{1,0:T(8,128)(2,1)S(1)} all-gather(bf16[128,128]{1,0:T(8,128)(2,1)} %get-tuple-element.11), channel_id=2, replica_groups=mesh['groups'=2,'z'=16,'core'=2,'tp'=8] {'z'}, dimensions={0}, use_global_device_ids=true | all-gather | bytes 557056 | tf_op jit(solution)/shard_map/all_gather | solution.py:147
  79.0 9.8 %collective-permute-start = (bf16[16,128,128]{2,1,0:T(8,128)(2,1)S(1)}, bf16[16,128,128]{2,1,0:T(8,128)(2,1)S(1)}, u32[]{:S(2)}, u32[]{:S(2)}) collective-permute-start(bf16[16,128,128]{2,1,0:T(8,128)(2,1)S(1)} %bitcast.5), channel_id=1, source_target_pairs={{0,8},{8,0},{1,9},{9,1},{2,10},{10,2},{3,11},{11,3},{4,12},{12,4},... | collective-permute-start | bytes 1572872 | tf_op jit(solution)/shard_map/ppermute | solution.py:148
  88.8 28.8 %all-gather.1 = bf16[2048,128]{1,0:T(8,128)(2,1)S(1)} all-gather(bf16[128,128]{1,0:T(8,128)(2,1)} %get-tuple-element.12), channel_id=3, replica_groups=mesh['groups'=2,'z'=16,'core'=2,'tp'=8] {'z'}, dimensions={0}, use_global_device_ids=true | all-gather | bytes 557056 | tf_op jit(solution)/shard_map/all_gather | solution.py:149
  117.5 6.5 %collective-permute-start.1 = (bf16[16,128,128]{2,1,0:T(8,128)(2,1)S(1)}, bf16[16,128,128]{2,1,0:T(8,128)(2,1)S(1)}, u32[]{:S(2)}, u32[]{:S(2)}) collective-permute-start(bf16[16,128,128]{2,1,0:T(8,128)(2,1)S(1)} %bitcast.7), channel_id=1, source_target_pairs={{0,8},{8,0},{1,9},{9,1},{2,10},{10,2},{3,11},{11,3},{4,12},{12,4},... | collective-permute-start | bytes 1572872 | tf_op jit(solution)/shard_map/ppermute | solution.py:150
  124.0 0.0 collective-permute-done.kb_ref
  124.0 1.5 collective-permute-done.1.vb_ref
  125.5 0.0 copy-start.1
  125.5 0.9 copy-done.1
  126.5 0.0 copy-start.2
  126.5 0.7 copy-done.2
  127.2 1.6 attend.1.a_ref
  128.8 0.0 copy-start
  128.8 0.7 copy-done
  129.5 0.0 all-gather.5.cloned.1.call-done
  129.5 6.0 %project.1 = bf16[8,128,512]{2,1,0:T(8,128)(2,1)} custom-call(bf16[128,1024]{1,0:T(8,128)(2,1)} %copy-done, bf16[32,1024,128]{2,1,0:T(8,128)(2,1)} %bitcast.9, bf16[32,1024,128]{2,1,0:T(8,128)(2,1)} %bitcast.10, bf16[32,1024,128]{2,1,0:T(8,128)(2,1)} %bitcast.11, bf16[32,1024,128]{2,1,0:T(8,128)(2,1)} %bitcast.12, bf16[32,1024,128]{2,1,0:T(8,128)(2,1)} %bitcast.13, ...), custom_call_target="tpu_custom_call" | custom-call | flops 1000000000 | bytes 10000000 | tf_op jit(solution)/shard_map/project/pallas_call | solution.py:171
  135.4 34.1 %all_to_all.5 = bf16[8,128,512]{2,1,0:T(8,128)(2,1)S(1)} all-to-all(bf16[8,128,512]{2,1,0:T(8,128)(2,1)} %project.1), channel_id=1, replica_groups=mesh['groups'=2,'z'=16,'core'=2,'tp'=8] {'tp'}, dimensions={0} | all-to-all | bytes 2097152 | tf_op jit(solution)/shard_map/all_to_all | solution.py:184
  169.6 0.8 reduce_sum.12
  (2 shorter events, 0.0 us)
Async XLA Ops:
  6.5 122.9 %all-gather.5.cloned.1.call-start = ((), (), s32[]{:S(2)}) async-start(), calls=%async_computation.1 | async-start | bytes 8650752 | tf_op jit(solution)/shard_map/all_gather | solution.py:121
  79.0 45.0 %collective-permute-start = (bf16[16,128,128]{2,1,0:T(8,128)(2,1)S(1)}, bf16[16,128,128]{2,1,0:T(8,128)(2,1)S(1)}, u32[]{:S(2)}, u32[]{:S(2)}) collective-permute-start(bf16[16,128,128]{2,1,0:T(8,128)(2,1)S(1)} %bitcast.5), channel_id=1, source_target_pairs={{0,8},{8,0},{1,9},{9,1},{2,10},{10,2},{3,11},{11,3},{4,12},{12,4},... | collective-permute-start | bytes 1572872 | tf_op jit(solution)/shard_map/ppermute | solution.py:148
  117.5 8.0 %collective-permute-start.1 = (bf16[16,128,128]{2,1,0:T(8,128)(2,1)S(1)}, bf16[16,128,128]{2,1,0:T(8,128)(2,1)S(1)}, u32[]{:S(2)}, u32[]{:S(2)}) collective-permute-start(bf16[16,128,128]{2,1,0:T(8,128)(2,1)S(1)} %bitcast.7), channel_id=1, source_target_pairs={{0,8},{8,0},{1,9},{9,1},{2,10},{10,2},{3,11},{11,3},{4,12},{12,4},... | collective-permute-start | bytes 1572872 | tf_op jit(solution)/shard_map/ppermute | solution.py:150
  125.5 0.9 copy-start.1
  126.5 0.7 copy-start.2
  128.8 0.7 copy-start
Sparse Core Ops, SparseCore 0:
  9.5 119.9 all-gather.4

commit v6 on v5

--- a/solution.py
+++ b/solution.py
@@ -25,25 +25,17 @@
     return jnp.cos(angles), jnp.where(lane < half_dim, -1.0, 1.0) * jnp.sin(angles)
 
 
-def prepare(heads, info, cosine_ref, sine_ref, q_hbm, k_hbm, v_hbm, doc_hbm, q_out, k_out, v_out, first_out, q_ref, k_ref, v_ref, doc_ref, sems):
-    pairs = ((k_hbm, k_ref), (v_hbm, v_ref), (q_hbm, q_ref), (doc_hbm, doc_ref))
-    copies = [pltpu.make_async_copy(a, b, sems.at[i]) for i, (a, b) in enumerate(pairs)]
-    for copy in copies:
-        copy.start()
+def prepare(heads, info, cosine_ref, sine_ref, q_ref, k_ref, v_ref, doc_ref, q_out, k_out, v_out, first_out):
     cosine, sine = cosine_ref[...], sine_ref[...]
 
     def turned(x):
         x = x.astype(jnp.float32)
         return (x * cosine + pltpu.roll(x, HEAD_SIZE // 2, 1) * sine).astype(jnp.bfloat16)
 
-    copies[0].wait()
     k_out[...] = turned(k_ref[...])
-    copies[1].wait()
     v_out[...] = v_ref[...].astype(jnp.float32).T.astype(jnp.bfloat16)
-    copies[2].wait()
     for h in range(heads):
         q_out[h] = turned(q_ref[:, h * HEAD_SIZE : (h + 1) * HEAD_SIZE])
-    copies[3].wait()
     docs, here = doc_ref[...], doc_ref[pl.ds(info[0], 1), :]
     first = jnp.zeros(here.shape, jnp.int32)
     for d in range(1, DOCS):
@@ -104,13 +96,20 @@
             ].T.astype(jnp.bfloat16)
 
 
-def project(count, parts, a_ref, *refs):
-    out_ref = refs[count]
-    width = out_ref.shape[2]
-    weights = jnp.concatenate([w_ref[0] for w_ref in refs[:count]], 1)
-    terms = jnp.dot(a_ref[...], weights, preferred_element_type=jnp.float32).astype(jnp.bfloat16)
-    for i in range(parts):
-        out_ref[i] = terms[:, i * width : (i + 1) * width]
+def project(share, a_ref, w_hbm, out_ref, w_ref, sems):
+    parts = out_ref.shape[0]
+    spans = [pl.ds(i * share, share) for i in range(parts)]
+    copies = [
+        pltpu.make_async_copy(w_hbm.at[at], w_ref.at[at], sems.at[i]) for i, at in enumerate(spans)
+    ]
+    for copy in copies:
+        copy.start()
+    for i, copy in enumerate(copies):
+        copy.wait()
+        weights = jnp.concatenate([w_ref[i * share + j] for j in range(share)], 1)
+        out_ref[i] = jnp.dot(a_ref[...], weights, preferred_element_type=jnp.float32).astype(
+            jnp.bfloat16
+        )
 
 
 def on_device(query_matrix, key_matrix, value_matrix, doc_ids, out_weight):
@@ -124,7 +123,6 @@
     docs = doc_ids.reshape(-1, tok_rows)
     vmem = pl.BlockSpec(memory_space=pltpu.VMEM)
     smem = pl.BlockSpec(memory_space=pltpu.SMEM)
-    hbm = pl.BlockSpec(memory_space=pltpu.HBM)
     small = pltpu.CompilerParams(vmem_limit_bytes=16 * 2**20)
     queries, keys_here, values_here, first = pl.pallas_call(
         functools.partial(prepare, query_heads),
@@ -134,12 +132,9 @@
             jax.ShapeDtypeStruct(value_matrix.shape[::-1], jnp.bfloat16),
             jax.ShapeDtypeStruct((8, tok_rows), jnp.int32),
         ),
-        in_specs=[smem, vmem, vmem] + [hbm] * 4,
+        in_specs=[smem] + [vmem] * 6,
         out_specs=(vmem,) * 4,
-        scratch_shapes=[
-            pltpu.VMEM(x.shape, x.dtype) for x in (query_matrix, key_matrix, value_matrix, docs)
-        ]
-        + [pltpu.SemaphoreType.DMA((4,))],
+        compiler_params=small,
         cost_estimate=pl.CostEstimate(flops=10**6, bytes_accessed=10**6, transcendentals=0),
         name="prepare",
     )(info, *rotary_tables(given_pos), query_matrix, key_matrix, value_matrix, docs)
@@ -148,7 +143,7 @@
     keys_b = lax.ppermute(keys_a, "core", swap)
     values_a = lax.all_gather(values_here, "z", axis=0, tiled=False)
     values_b = lax.ppermute(values_a, "core", swap)
-    together = math.gcd(query_heads, 2)
+    together = 1
     sets = query_heads // together
     attention = pl.pallas_call(
         functools.partial(attend, query_heads, together),
@@ -166,21 +161,19 @@
     )(info, first, queries, keys_a, keys_b, values_a, values_b)
     blocks, depth, width = weight_blocks.shape
     share = blocks // members
-    parts = math.gcd(members, 2)
-    count = share * parts
     terms = pl.pallas_call(
-        functools.partial(project, count, parts),
-        grid=(blocks // count,),
+        functools.partial(project, share),
         out_shape=jax.ShapeDtypeStruct((members, tok_rows, share * width), jnp.bfloat16),
-        in_specs=[pl.BlockSpec((tok_rows, depth), lambda i: (0, 0))]
-        + [
-            pl.BlockSpec((1, depth, width), lambda i, j=j: (i * count + j, 0, 0))
-            for j in range(count)
+        in_specs=[vmem, pl.BlockSpec(memory_space=pl.ANY)],
+        out_specs=vmem,
+        scratch_shapes=[
+            pltpu.VMEM(weight_blocks.shape, jnp.bfloat16),
+            pltpu.SemaphoreType.DMA((members,)),
         ],
-        out_specs=pl.BlockSpec((parts, tok_rows, share * width), lambda i: (i, 0, 0)),
+        compiler_params=pltpu.CompilerParams(vmem_limit_bytes=58 * 2**20),
         cost_estimate=pl.CostEstimate(flops=10**9, bytes_accessed=10**7, transcendentals=0),
         name="project",
-    )(attention, *[weight_blocks] * count)
+    )(attention, weight_blocks)
     arrived = lax.all_to_all(terms, "tp", split_axis=0, concat_axis=0, tiled=True)
     return arrived.astype(jnp.float32).sum(axis=0).astype(jnp.bfloat16)
 

time: 178 us -> 178 us (level)
  Pallas kernels: 10.3 us -> 7.24 us
  blocking collectives: 131 us -> 133 us
  waiting for transfers between devices: 2.26 us -> 4.14 us
    pallas_call x1, Pallas kernels: 2.78 us -> 0.23 us  [on_device(): pl.pallas_call(functools.partial(prepare, query_heads), out_shape=(jax.Sh...]
    all_gather x1, waiting for transfers between devices: 0.01 us -> 1.89 us  [on_device(): lax.all_gather(out_weight, ('z', 'core'), axis=0, tiled=False)]
    unnamed x6 -> x10, local copies, waits for them, and re-layouts: 2.31 us -> 3.87 us
  transfers between devices with their start and end apart: 3 -> 3, of which waited for: 1 -> 2; matrix products, arithmetic and copies ran while one was open for 1% -> 0% of each run, Pallas kernels for 2% -> 1%
where the time goes in v6:
time: 178 us
  blocking collectives  133 us (75%)
  starting transfers between devices  15.4 us (9%)
  between operations  13.5 us (8%)
  Pallas kernels  7.24 us (4%)
  waiting for transfers between devices  4.14 us (2%)
  local copies, waits for them, and re-layouts  3.87 us (2%)
    all_gather x1, blocking collectives, on_device(): keys_a = lax.all_gather(keys_here, 'z', axis=0, tiled=False)  67.5 us
    all_to_all x1, blocking collectives, on_device(): lax.all_to_all(terms, 'tp', split_axis=0, concat_axis=0, tiled=True)  35.7 us
    all_gather x1, blocking collectives, on_device(): values_a = lax.all_gather(values_here, 'z', axis=0, tiled=False)  29.5 us
    ppermute x1, starting transfers between devices, on_device(): keys_b = lax.ppermute(keys_a, 'core', swap)  9.76 us
    pallas_call x1, Pallas kernels, on_device(): pl.pallas_call(functools.partial(project, share), out_shape=jax.ShapeDtyp...  5.82 us
    ppermute x1, starting transfers between devices, on_device(): values_b = lax.ppermute(values_a, 'core', swap)  5.6 us
    unnamed x10, local copies, waits for them, and re-layouts  3.87 us
  transfers between devices with their start and end apart: 3, of which 2 were waited for; matrix products, arithmetic and copies ran while one was open for 0% of the time, Pallas kernels for 1%

profile of v6, /device:TPU:65, one launch (start us, length us, event | category | flops | bytes accessed | tf_op | source)
XLA Modules:
  0.0 177.9 jit_solution(6866750937772197290)
XLA Ops:
  6.5 0.0 all-gather.5.cloned.1.call-start
  6.6 0.7 all-gather.5.cloned.1.call-update
  7.3 0.3 fusion
  7.7 0.0 copy-start.1
  7.7 0.9 copy-done.1
  8.6 0.0 copy-start.2
  8.6 0.8 copy-done.2
  9.4 0.0 copy-start.3
  9.4 0.8 copy-done.3
  10.1 0.0 copy-start.4
  10.1 0.7 copy-done.4
  10.8 0.2 prepare.1
  11.1 67.5 %all-gather = bf16[2048,128]{1,0:T(8,128)(2,1)S(1)} all-gather(bf16[128,128]{1,0:T(8,128)(2,1)S(1)} %get-tuple-element.11), channel_id=2, replica_groups=mesh['groups'=2,'z'=16,'core'=2,'tp'=8] {'z'}, dimensions={0}, use_global_device_ids=true | all-gather | bytes 557056 | tf_op jit(solution)/shard_map/all_gather | solution.py:142
  78.6 9.8 %collective-permute-start = (bf16[16,128,128]{2,1,0:T(8,128)(2,1)S(1)}, bf16[16,128,128]{2,1,0:T(8,128)(2,1)S(1)}, u32[]{:S(2)}, u32[]{:S(2)}) collective-permute-start(bf16[16,128,128]{2,1,0:T(8,128)(2,1)S(1)} %bitcast.5), channel_id=1, source_target_pairs={{0,8},{8,0},{1,9},{9,1},{2,10},{10,2},{3,11},{11,3},{4,12},{12,4},... | collective-permute-start | bytes 1572872 | tf_op jit(solution)/shard_map/ppermute | solution.py:143
  88.3 29.5 %all-gather.1 = bf16[2048,128]{1,0:T(8,128)(2,1)S(1)} all-gather(bf16[128,128]{1,0:T(8,128)(2,1)S(1)} %get-tuple-element.12), channel_id=3, replica_groups=mesh['groups'=2,'z'=16,'core'=2,'tp'=8] {'z'}, dimensions={0}, use_global_device_ids=true | all-gather | bytes 557056 | tf_op jit(solution)/shard_map/all_gather | solution.py:144
  117.8 5.6 %collective-permute-start.1 = (bf16[16,128,128]{2,1,0:T(8,128)(2,1)S(1)}, bf16[16,128,128]{2,1,0:T(8,128)(2,1)S(1)}, u32[]{:S(2)}, u32[]{:S(2)}) collective-permute-start(bf16[16,128,128]{2,1,0:T(8,128)(2,1)S(1)} %bitcast.7), channel_id=1, source_target_pairs={{0,8},{8,0},{1,9},{9,1},{2,10},{10,2},{3,11},{11,3},{4,12},{12,4},... | collective-permute-start | bytes 1572872 | tf_op jit(solution)/shard_map/ppermute | solution.py:145
  123.4 0.0 collective-permute-done.kb_ref
  123.4 1.5 collective-permute-done.1.vb_ref
  124.9 1.2 attend.1.a_ref
  126.1 0.0 copy-start
  126.1 0.7 copy-done
  126.8 1.9 %all-gather.5.cloned.1.call-done = bf16[32768,128]{1,0:T(8,128)(2,1)} async-done(((bf16[1024,128]{1,0:T(8,128)(2,1)}), bf16[32768,128]{1,0:T(8,128)(2,1)}) %all-gather.5.cloned.1.call-update) | async-done | bytes 8388624 | tf_op jit(solution)/shard_map/all_gather | solution.py:120
  128.7 5.8 %project.1 = bf16[8,128,512]{2,1,0:T(8,128)(2,1)} custom-call(bf16[128,1024]{1,0:T(8,128)(2,1)} %copy-done, bf16[32,1024,128]{2,1,0:T(8,128)(2,1)} %bitcast.10), custom_call_target="tpu_custom_call" | custom-call | flops 1000000000 | bytes 10000000 | tf_op jit(solution)/shard_map/project/pallas_call | solution.py:164
  134.5 35.7 %all_to_all.5 = bf16[8,128,512]{2,1,0:T(8,128)(2,1)S(1)} all-to-all(bf16[8,128,512]{2,1,0:T(8,128)(2,1)} %project.1), channel_id=1, replica_groups=mesh['groups'=2,'z'=16,'core'=2,'tp'=8] {'tp'}, dimensions={0} | all-to-all | bytes 2097152 | tf_op jit(solution)/shard_map/all_to_all | solution.py:177
  170.3 0.8 reduce_sum.12
  (2 shorter events, 0.0 us)
Async XLA Ops:
  6.5 122.2 %all-gather.5.cloned.1.call-start = ((), (), s32[]{:S(2)}) async-start(), calls=%async_computation.1 | async-start | bytes 8650752 | tf_op jit(solution)/shard_map/all_gather | solution.py:120
  7.7 1.0 copy-start.1
  8.6 0.8 copy-start.2
  9.4 0.8 copy-start.3
  10.1 0.7 copy-start.4
  78.6 44.9 %collective-permute-start = (bf16[16,128,128]{2,1,0:T(8,128)(2,1)S(1)}, bf16[16,128,128]{2,1,0:T(8,128)(2,1)S(1)}, u32[]{:S(2)}, u32[]{:S(2)}) collective-permute-start(bf16[16,128,128]{2,1,0:T(8,128)(2,1)S(1)} %bitcast.5), channel_id=1, source_target_pairs={{0,8},{8,0},{1,9},{9,1},{2,10},{10,2},{3,11},{11,3},{4,12},{12,4},... | collective-permute-start | bytes 1572872 | tf_op jit(solution)/shard_map/ppermute | solution.py:143
  117.8 7.1 %collective-permute-start.1 = (bf16[16,128,128]{2,1,0:T(8,128)(2,1)S(1)}, bf16[16,128,128]{2,1,0:T(8,128)(2,1)S(1)}, u32[]{:S(2)}, u32[]{:S(2)}) collective-permute-start(bf16[16,128,128]{2,1,0:T(8,128)(2,1)S(1)} %bitcast.7), channel_id=1, source_target_pairs={{0,8},{8,0},{1,9},{9,1},{2,10},{10,2},{3,11},{11,3},{4,12},{12,4},... | collective-permute-start | bytes 1572872 | tf_op jit(solution)/shard_map/ppermute | solution.py:145
  126.1 0.7 copy-start
Sparse Core Ops, SparseCore 0:
  9.5 119.1 all-gather.4

commit v7 on v6

--- a/solution.py
+++ b/solution.py
@@ -11,6 +11,7 @@
 
 HEAD_SIZE = 128
 CORES = 2
+REST = 8
 DOCS = 6
 
 
@@ -25,15 +26,20 @@
     return jnp.cos(angles), jnp.where(lane < half_dim, -1.0, 1.0) * jnp.sin(angles)
 
 
-def prepare(heads, info, cosine_ref, sine_ref, q_ref, k_ref, v_ref, doc_ref, q_out, k_out, v_out, first_out):
+def prepare(heads, info, cosine_ref, sine_ref, q_ref, k_ref, v_ref, doc_ref, q_out, kv_out, rest_out, first_out):
     cosine, sine = cosine_ref[...], sine_ref[...]
 
     def turned(x):
         x = x.astype(jnp.float32)
         return (x * cosine + pltpu.roll(x, HEAD_SIZE // 2, 1) * sine).astype(jnp.bfloat16)
 
-    k_out[...] = turned(k_ref[...])
-    v_out[...] = v_ref[...].astype(jnp.float32).T.astype(jnp.bfloat16)
+    rows = k_ref.shape[0]
+    values = v_ref[...].astype(jnp.float32).T
+    kept = kv_out.shape[0] - rows
+    kv_out[:rows] = turned(k_ref[...])
+    kv_out[rows:] = values[:kept].astype(jnp.bfloat16)
+    for i in range(rest_out.shape[0]):
+        rest_out[i] = values[kept:].astype(jnp.bfloat16)
     for h in range(heads):
         q_out[h] = turned(q_ref[:, h * HEAD_SIZE : (h + 1) * HEAD_SIZE])
     docs, here = doc_ref[...], doc_ref[pl.ds(info[0], 1), :]
@@ -44,8 +50,8 @@
     first_out[...] = jnp.broadcast_to(first, first_out.shape)
 
 
-def attend(heads, together, info, first_ref, q_ref, ka_ref, kb_ref, va_ref, vb_ref, out_ref, m_ref, l_ref, acc_ref):
-    rows = ka_ref.shape[1]
+def attend(heads, together, info, first_ref, q_ref, a_ref, b_ref, resta_ref, restb_ref, out_ref, m_ref, l_ref, acc_ref):
+    rows = out_ref.shape[0]
     ctx = info[0]
     core = lax.rem(ctx, CORES)
     chip = lax.div(ctx, CORES)
@@ -67,8 +73,10 @@
         position = key + jnp.where(mine, own, other)
         bias = jnp.where((position >= first) & (position <= given), 0.0, -1e30)
         bias = jnp.concatenate([bias] * together, 1)
-        keys = jnp.concatenate([ka_ref[at], kb_ref[at]], 0)
-        values = jnp.concatenate([va_ref[at], vb_ref[at]], 1)
+        keys = jnp.concatenate([a_ref[at, :rows], b_ref[at, :rows]], 0)
+        most = jnp.concatenate([a_ref[at, rows:], b_ref[at, rows:]], 1)
+        rest = jnp.concatenate([resta_ref[at], restb_ref[at]], 1)
+        values = jnp.concatenate([most, rest], 0)
         for g in range(heads // together):
             q = q_ref[g * together : (g + 1) * together].reshape(together * rows, HEAD_SIZE)
             scores = lax.dot_general(
@@ -124,12 +132,13 @@
     vmem = pl.BlockSpec(memory_space=pltpu.VMEM)
     smem = pl.BlockSpec(memory_space=pltpu.SMEM)
     small = pltpu.CompilerParams(vmem_limit_bytes=16 * 2**20)
-    queries, keys_here, values_here, first = pl.pallas_call(
+    chips = lax.axis_size("z")
+    queries, here, rest_here, first = pl.pallas_call(
         functools.partial(prepare, query_heads),
         out_shape=(
             jax.ShapeDtypeStruct((query_heads, tok_rows, HEAD_SIZE), jnp.bfloat16),
-            jax.ShapeDtypeStruct(key_matrix.shape, jnp.bfloat16),
-            jax.ShapeDtypeStruct(value_matrix.shape[::-1], jnp.bfloat16),
+            jax.ShapeDtypeStruct((tok_rows + HEAD_SIZE - REST, HEAD_SIZE), jnp.bfloat16),
+            jax.ShapeDtypeStruct((chips, REST, tok_rows), jnp.bfloat16),
             jax.ShapeDtypeStruct((8, tok_rows), jnp.int32),
         ),
         in_specs=[smem] + [vmem] * 6,
@@ -139,10 +148,10 @@
         name="prepare",
     )(info, *rotary_tables(given_pos), query_matrix, key_matrix, value_matrix, docs)
     swap = [(i, CORES - 1 - i) for i in range(CORES)]
-    keys_a = lax.all_gather(keys_here, "z", axis=0, tiled=False)
-    keys_b = lax.ppermute(keys_a, "core", swap)
-    values_a = lax.all_gather(values_here, "z", axis=0, tiled=False)
-    values_b = lax.ppermute(values_a, "core", swap)
+    most_a = lax.all_gather(here, "z", axis=0, tiled=False)
+    most_b = lax.ppermute(most_a, "core", swap)
+    rest_a = lax.all_to_all(rest_here, "z", split_axis=0, concat_axis=0, tiled=True)
+    rest_b = lax.ppermute(rest_a, "core", swap)
     together = 1
     sets = query_heads // together
     attention = pl.pallas_call(
@@ -158,7 +167,7 @@
         cost_estimate=pl.CostEstimate(flops=2 * 10**9, bytes_accessed=3 * 10**6, transcendentals=10**6),
         compiler_params=small,
         name="attend",
-    )(info, first, queries, keys_a, keys_b, values_a, values_b)
+    )(info, first, queries, most_a, most_b, rest_a, rest_b)
     blocks, depth, width = weight_blocks.shape
     share = blocks // members
     terms = pl.pallas_call(

time: 178 us -> 178 us (level)
  waiting for transfers between devices: 4.14 us -> 13.6 us
  blocking collectives: 133 us -> 124 us
    all_gather x2 -> x1, blocking collectives: 97 us -> 72.5 us  [on_device(): most_a = lax.all_gather(here, 'z', axis=0, tiled=False)]
    all_to_all x0 -> x1, blocking collectives: none -> 15.5 us  [on_device(): lax.all_to_all(rest_here, 'z', split_axis=0, concat_axis=0, tiled=True)]
    all_gather x1, waiting for transfers between devices: 1.89 us -> 12 us  [on_device(): lax.all_gather(out_weight, ('z', 'core'), axis=0, tiled=False)]
where the time goes in v7:
time: 178 us; the launch traced here: 177 us
  blocking collectives  124 us (70%)
  starting transfers between devices  14.1 us (8%)
  waiting for transfers between devices  13.6 us (8%)
  between operations  13.5 us (8%)
  Pallas kernels  7.24 us (4%)
  local copies, waits for them, and re-layouts  3.87 us (2%)
    all_gather x1, blocking collectives, on_device(): most_a = lax.all_gather(here, 'z', axis=0, tiled=False)  72.5 us
    all_to_all x1, blocking collectives, on_device(): lax.all_to_all(terms, 'tp', split_axis=0, concat_axis=0, tiled=True)  36.1 us
    all_to_all x1, blocking collectives, on_device(): lax.all_to_all(rest_here, 'z', split_axis=0, concat_axis=0, tiled=True)  15.5 us
    all_gather x1, waiting for transfers between devices, on_device(): lax.all_gather(out_weight, ('z', 'core'), axis=0, tiled=False)  12 us
    ppermute x1, starting transfers between devices, on_device(): most_b = lax.ppermute(most_a, 'core', swap)  10.5 us
    pallas_call x1, Pallas kernels, on_device(): pl.pallas_call(functools.partial(project, share), out_shape=jax.ShapeDtyp...  5.82 us
    unnamed x10, local copies, waits for them, and re-layouts  3.87 us
    ppermute x1, starting transfers between devices, on_device(): rest_b = lax.ppermute(rest_a, 'core', swap)  3.58 us
  transfers between devices with their start and end apart: 3, of which 2 were waited for; matrix products, arithmetic and copies ran while one was open for 0% of the time, Pallas kernels for 1%

profile of v7, /device:TPU:65, one launch (start us, length us, event | category | flops | bytes accessed | tf_op | source)
XLA Modules:
  0.0 177.5 jit_solution(5504613419425837868)
XLA Ops:
  6.5 0.0 all-gather.4.cloned.1.call-start
  6.6 0.7 all-gather.4.cloned.1.call-update
  7.3 0.3 fusion
  7.7 0.0 copy-start.1
  7.7 0.9 copy-done.1
  8.6 0.0 copy-start.2
  8.6 0.8 copy-done.2
  9.4 0.0 copy-start.3
  9.4 0.8 copy-done.3
  10.1 0.0 copy-start.4
  10.1 0.7 copy-done.4
  10.8 0.2 prepare.1
  11.1 72.5 %all-gather = bf16[3968,128]{1,0:T(8,128)(2,1)S(1)} all-gather(bf16[248,128]{1,0:T(8,128)(2,1)S(1)} %get-tuple-element.11), channel_id=2, replica_groups=mesh['groups'=2,'z'=16,'core'=2,'tp'=8] {'z'}, dimensions={0}, use_global_device_ids=true | all-gather | bytes 1079296 | tf_op jit(solution)/shard_map/all_gather | solution.py:151
  83.6 10.5 %collective-permute-start = (bf16[16,248,128]{2,1,0:T(8,128)(2,1)S(1)}, bf16[16,248,128]{2,1,0:T(8,128)(2,1)S(1)}, u32[]{:S(2)}, u32[]{:S(2)}) collective-permute-start(bf16[16,248,128]{2,1,0:T(8,128)(2,1)S(1)} %bitcast.4), channel_id=1, source_target_pairs={{0,8},{8,0},{1,9},{9,1},{2,10},{10,2},{3,11},{11,3},{4,12},{12,4},... | collective-permute-start | bytes 3047432 | tf_op jit(solution)/shard_map/ppermute | solution.py:152
  94.2 15.5 %all_to_all.10.resta_ref = bf16[16,8,128]{2,1,0:T(8,128)(2,1)S(1)} all-to-all(bf16[16,8,128]{2,1,0:T(8,128)(2,1)S(1)} %get-tuple-element.12), channel_id=1, replica_groups=mesh['groups'=2,'z'=16,'core'=2,'tp'=8] {'z'}, dimensions={0} | all-to-all | bytes 65536 | tf_op jit(solution)/shard_map/all_to_all | solution.py:153
  109.6 3.6 %collective-permute-start.1 = (bf16[16,8,128]{2,1,0:T(8,128)(2,1)S(1)}, bf16[16,8,128]{2,1,0:T(8,128)(2,1)S(1)}, u32[]{:S(2)}, u32[]{:S(2)}) collective-permute-start(bf16[16,8,128]{2,1,0:T(8,128)(2,1)S(1)} %all_to_all.10.resta_ref), channel_id=1, source_target_pairs={{0,8},{8,0},{1,9},{9,1},{2,10},{10,2},{3,11},{11,3},{4,12},{12,4},... | collective-permute-start | bytes 98312 | tf_op jit(solution)/shard_map/ppermute | solution.py:154
  113.2 0.8 collective-permute-done.1.restb_ref
  114.0 0.0 collective-permute-done.b_ref
  114.0 1.2 attend.1.a_ref
  115.2 0.0 copy-start
  115.2 0.7 copy-done
  115.9 12.0 %all-gather.4.cloned.1.call-done = bf16[32768,128]{1,0:T(8,128)(2,1)} async-done(((bf16[1024,128]{1,0:T(8,128)(2,1)}), bf16[32768,128]{1,0:T(8,128)(2,1)}) %all-gather.4.cloned.1.call-update) | async-done | bytes 8388624 | tf_op jit(solution)/shard_map/all_gather | solution.py:128
  127.9 5.8 %project.1 = bf16[8,128,512]{2,1,0:T(8,128)(2,1)} custom-call(bf16[128,1024]{1,0:T(8,128)(2,1)} %copy-done, bf16[32,1024,128]{2,1,0:T(8,128)(2,1)} %bitcast.7), custom_call_target="tpu_custom_call" | custom-call | flops 1000000000 | bytes 10000000 | tf_op jit(solution)/shard_map/project/pallas_call | solution.py:173
  133.7 36.1 %all_to_all.11 = bf16[8,128,512]{2,1,0:T(8,128)(2,1)S(1)} all-to-all(bf16[8,128,512]{2,1,0:T(8,128)(2,1)} %project.1), channel_id=1, replica_groups=mesh['groups'=2,'z'=16,'core'=2,'tp'=8] {'tp'}, dimensions={0} | all-to-all | bytes 2097152 | tf_op jit(solution)/shard_map/all_to_all | solution.py:186
  169.8 0.8 reduce_sum.12
  (2 shorter events, 0.0 us)
Async XLA Ops:
  6.5 121.4 %all-gather.4.cloned.1.call-start = ((), (), s32[]{:S(2)}) async-start(), calls=%async_computation.2 | async-start | bytes 8650752 | tf_op jit(solution)/shard_map/all_gather | solution.py:128
  7.7 1.0 copy-start.1
  8.6 0.8 copy-start.2
  9.4 0.8 copy-start.3
  10.1 0.7 copy-start.4
  83.6 30.4 %collective-permute-start = (bf16[16,248,128]{2,1,0:T(8,128)(2,1)S(1)}, bf16[16,248,128]{2,1,0:T(8,128)(2,1)S(1)}, u32[]{:S(2)}, u32[]{:S(2)}) collective-permute-start(bf16[16,248,128]{2,1,0:T(8,128)(2,1)S(1)} %bitcast.4), channel_id=1, source_target_pairs={{0,8},{8,0},{1,9},{9,1},{2,10},{10,2},{3,11},{11,3},{4,12},{12,4},... | collective-permute-start | bytes 3047432 | tf_op jit(solution)/shard_map/ppermute | solution.py:152
  109.6 4.4 %collective-permute-start.1 = (bf16[16,8,128]{2,1,0:T(8,128)(2,1)S(1)}, bf16[16,8,128]{2,1,0:T(8,128)(2,1)S(1)}, u32[]{:S(2)}, u32[]{:S(2)}) collective-permute-start(bf16[16,8,128]{2,1,0:T(8,128)(2,1)S(1)} %all_to_all.10.resta_ref), channel_id=1, source_target_pairs={{0,8},{8,0},{1,9},{9,1},{2,10},{10,2},{3,11},{11,3},{4,12},{12,4},... | collective-permute-start | bytes 98312 | tf_op jit(solution)/shard_map/ppermute | solution.py:154
  115.2 0.7 copy-start
Sparse Core Ops, SparseCore 0:
  9.5 118.3 all-gather.3

commit v8 on v7

--- a/solution.py
+++ b/solution.py
@@ -104,7 +104,7 @@
             ].T.astype(jnp.bfloat16)
 
 
-def project(share, a_ref, w_hbm, out_ref, w_ref, sems):
+def project(share, own_ref, other_ref, w_hbm, out_ref, w_ref, sems):
     parts = out_ref.shape[0]
     spans = [pl.ds(i * share, share) for i in range(parts)]
     copies = [
@@ -112,20 +112,39 @@
     ]
     for copy in copies:
         copy.start()
+    both = jnp.concatenate([own_ref[...], other_ref[...]], 0)
     for i, copy in enumerate(copies):
         copy.wait()
         weights = jnp.concatenate([w_ref[i * share + j] for j in range(share)], 1)
-        out_ref[i] = jnp.dot(a_ref[...], weights, preferred_element_type=jnp.float32).astype(
+        out_ref[i] = jnp.dot(both, weights, preferred_element_type=jnp.float32).astype(
             jnp.bfloat16
         )
+
+
+def total(terms_ref, kept_ref, sent_ref):
+    rows = kept_ref.shape[0]
+    for i, out_ref in enumerate((kept_ref, sent_ref)):
+        at = slice(i * rows, (i + 1) * rows)
+        out_ref[...] = jnp.sum(terms_ref[:, at].astype(jnp.float32), 0).astype(jnp.bfloat16)
+
+
+def weave(count, core, kept_ref, given_ref, out_ref):
+    width = kept_ref.shape[1] // count
+    even = core[0] == 0
+    for j in range(count):
+        kept, given = (r[:, j * width : (j + 1) * width] for r in (kept_ref, given_ref))
+        at = j * CORES * width
+        out_ref[:, at : at + width] = jnp.where(even, kept, given)
+        out_ref[:, at + width : at + CORES * width] = jnp.where(even, given, kept)
 
 
 def on_device(query_matrix, key_matrix, value_matrix, doc_ids, out_weight):
     tok_rows = query_matrix.shape[0]
     query_heads = query_matrix.shape[1] // HEAD_SIZE
     members = lax.axis_size("tp")
-    ctx_index = lax.axis_index("z") * CORES + lax.axis_index("core")
-    weight_blocks = lax.all_gather(out_weight, ("z", "core"), axis=0, tiled=False)
+    core = lax.axis_index("core")
+    ctx_index = lax.axis_index("z") * CORES + core
+    weight_blocks = lax.all_gather(out_weight, "z", axis=0, tiled=False)
     given_pos = ctx_index * tok_rows + jnp.arange(tok_rows, dtype=jnp.int32)
     info = ctx_index.astype(jnp.int32).reshape(1)
     docs = doc_ids.reshape(-1, tok_rows)
@@ -168,23 +187,41 @@
         compiler_params=small,
         name="attend",
     )(info, first, queries, most_a, most_b, rest_a, rest_b)
+    attention_other = lax.ppermute(attention, "core", swap)
     blocks, depth, width = weight_blocks.shape
     share = blocks // members
     terms = pl.pallas_call(
         functools.partial(project, share),
-        out_shape=jax.ShapeDtypeStruct((members, tok_rows, share * width), jnp.bfloat16),
-        in_specs=[vmem, pl.BlockSpec(memory_space=pl.ANY)],
+        out_shape=jax.ShapeDtypeStruct((members, CORES * tok_rows, share * width), jnp.bfloat16),
+        in_specs=[vmem, vmem, pl.BlockSpec(memory_space=pltpu.HBM)],
         out_specs=vmem,
         scratch_shapes=[
             pltpu.VMEM(weight_blocks.shape, jnp.bfloat16),
             pltpu.SemaphoreType.DMA((members,)),
         ],
-        compiler_params=pltpu.CompilerParams(vmem_limit_bytes=58 * 2**20),
+        compiler_params=pltpu.CompilerParams(vmem_limit_bytes=59 * 2**20),
         cost_estimate=pl.CostEstimate(flops=10**9, bytes_accessed=10**7, transcendentals=0),
         name="project",
-    )(attention, weight_blocks)
+    )(attention, attention_other, weight_blocks)
     arrived = lax.all_to_all(terms, "tp", split_axis=0, concat_axis=0, tiled=True)
-    return arrived.astype(jnp.float32).sum(axis=0).astype(jnp.bfloat16)
+    half = jax.ShapeDtypeStruct((tok_rows, share * width), jnp.bfloat16)
+    kept, sent = pl.pallas_call(
+        total,
+        out_shape=(half, half),
+        in_specs=[vmem],
+        out_specs=(vmem, vmem),
+        compiler_params=small,
+        name="total",
+    )(arrived)
+    given = lax.ppermute(sent, "core", swap)
+    return pl.pallas_call(
+        functools.partial(weave, share),
+        out_shape=jax.ShapeDtypeStruct((tok_rows, share * CORES * width), jnp.bfloat16),
+        in_specs=[pl.BlockSpec(memory_space=pltpu.SMEM), vmem, vmem],
+        out_specs=vmem,
+        compiler_params=small,
+        name="weave",
+    )(core.astype(jnp.int32).reshape(1), kept, given)
 
 
 def solution(mesh):

time: 178 us -> 174 us (0.978)
  starting transfers between devices: 14.1 us -> 26.9 us
  waiting for transfers between devices: 13.6 us -> 5.01 us
  blocking collectives: 124 us -> 116 us
    ppermute x0 -> x2, starting transfers between devices: none -> 13.9 us  [the longest x1 11.6 us: on_device(): given = lax.ppermute(sent, 'core', swap)]
    all_gather x1, waiting for transfers between devices: 12 us -> 1.37 us  [on_device(): weight_blocks = lax.all_gather(out_weight, 'z', axis=0, tiled=False)]
    all_to_all x1, blocking collectives: 36.1 us -> 27 us  [on_device(): lax.all_to_all(terms, 'tp', split_axis=0, concat_axis=0, tiled=True)]
    ppermute x0 -> x2, waiting for transfers between devices: none -> 2.05 us  [the longest x1 1.17 us: on_device(): attention_other = lax.ppermute(attention, 'core', swap)]
    unnamed x10 -> x12, local copies, waits for them, and re-layouts: 3.87 us -> 3.18 us
  transfers between devices with their start and end apart: 3 -> 5, of which waited for: 2 -> 4; matrix products, arithmetic and copies ran while one was open for 0% -> 0% of each run, Pallas kernels for 1% -> 1%
where the time goes in v8:
time: 174 us
  blocking collectives  116 us (67%)
  starting transfers between devices  26.9 us (15%)
  between operations  13.5 us (8%)
  Pallas kernels  8.72 us (5%)
  waiting for transfers between devices  5.01 us (3%)
  local copies, waits for them, and re-layouts  3.18 us (2%)
    all_gather x1, blocking collectives, on_device(): most_a = lax.all_gather(here, 'z', axis=0, tiled=False)  73.1 us
    all_to_all x1, blocking collectives, on_device(): lax.all_to_all(terms, 'tp', split_axis=0, concat_axis=0, tiled=True)  27 us
    all_to_all x1, blocking collectives, on_device(): lax.all_to_all(rest_here, 'z', split_axis=0, concat_axis=0, tiled=True)  15.9 us
    ppermute x1, starting transfers between devices, on_device(): given = lax.ppermute(sent, 'core', swap)  11.6 us
    ppermute x1, starting transfers between devices, on_device(): most_b = lax.ppermute(most_a, 'core', swap)  9.74 us
    pallas_call x1, Pallas kernels, on_device(): pl.pallas_call(functools.partial(project, share), out_shape=jax.ShapeDtyp...  6.49 us
  transfers between devices with their start and end apart: 5, of which 4 were waited for; matrix products, arithmetic and copies ran while one was open for 0% of the time, Pallas kernels for 1%

profile of v8, /device:TPU:65, one launch (start us, length us, event | category | flops | bytes accessed | tf_op | source)
XLA Modules:
  0.0 173.7 jit_solution(11173316133597619482)
XLA Ops:
  6.5 0.0 all-gather.4.cloned.1.call-start
  6.6 0.7 all-gather.4.cloned.1.call-update
  7.3 0.3 fusion
  7.7 0.0 copy-start.1
  7.7 0.9 copy-done.1
  8.6 0.0 copy-start.2
  8.6 0.8 copy-done.2
  9.4 0.0 copy-start.3
  9.4 0.8 copy-done.3
  10.1 0.0 copy-start.4
  10.1 0.7 copy-done.4
  10.8 0.2 prepare.1
  11.1 73.1 %all-gather = bf16[3968,128]{1,0:T(8,128)(2,1)S(1)} all-gather(bf16[248,128]{1,0:T(8,128)(2,1)S(1)} %get-tuple-element.13), channel_id=2, replica_groups=mesh['groups'=2,'z'=16,'core'=2,'tp'=8] {'z'}, dimensions={0}, use_global_device_ids=true | all-gather | bytes 1079296 | tf_op jit(solution)/shard_map/all_gather | solution.py:170
  84.2 9.7 %collective-permute-start = (bf16[16,248,128]{2,1,0:T(8,128)(2,1)S(1)}, bf16[16,248,128]{2,1,0:T(8,128)(2,1)S(1)}, u32[]{:S(2)}, u32[]{:S(2)}) collective-permute-start(bf16[16,248,128]{2,1,0:T(8,128)(2,1)S(1)} %bitcast.5), channel_id=1, source_target_pairs={{0,8},{8,0},{1,9},{9,1},{2,10},{10,2},{3,11},{11,3},{4,12},{12,4},... | collective-permute-start | bytes 3047432 | tf_op jit(solution)/shard_map/ppermute | solution.py:171
  93.9 15.9 %all_to_all.10.resta_ref = bf16[16,8,128]{2,1,0:T(8,128)(2,1)S(1)} all-to-all(bf16[16,8,128]{2,1,0:T(8,128)(2,1)S(1)} %get-tuple-element.14), channel_id=1, replica_groups=mesh['groups'=2,'z'=16,'core'=2,'tp'=8] {'z'}, dimensions={0} | all-to-all | bytes 65536 | tf_op jit(solution)/shard_map/all_to_all | solution.py:172
  109.9 3.2 %collective-permute-start.1 = (bf16[16,8,128]{2,1,0:T(8,128)(2,1)S(1)}, bf16[16,8,128]{2,1,0:T(8,128)(2,1)S(1)}, u32[]{:S(2)}, u32[]{:S(2)}) collective-permute-start(bf16[16,8,128]{2,1,0:T(8,128)(2,1)S(1)} %all_to_all.10.resta_ref), channel_id=1, source_target_pairs={{0,8},{8,0},{1,9},{9,1},{2,10},{10,2},{3,11},{11,3},{4,12},{12,4},... | collective-permute-start | bytes 98312 | tf_op jit(solution)/shard_map/ppermute | solution.py:173
  113.1 0.8 collective-permute-done.1.restb_ref
  114.0 0.0 collective-permute-done.b_ref
  114.0 1.2 attend.1.own_ref
  115.2 0.0 copy-start
  115.2 2.3 %collective-permute-start.2 = (bf16[128,1024]{1,0:T(8,128)(2,1)S(1)}, bf16[128,1024]{1,0:T(8,128)(2,1)S(1)}, u32[]{:S(2)}, u32[]{:S(2)}) collective-permute-start(bf16[128,1024]{1,0:T(8,128)(2,1)S(1)} %attend.1.own_ref), channel_id=1, source_target_pairs={{0,8},{8,0},{1,9},{9,1},{2,10},{10,2},{3,11},{11,3},{4,12},{12,4},... | collective-permute-start | bytes 786440 | tf_op jit(solution)/shard_map/ppermute | solution.py:190
  117.5 1.2 collective-permute-done.2.other_ref
  118.6 0.0 copy-start.5
  118.6 1.4 all-gather.4.cloned.1.call-done
  120.0 0.0 copy-done
  120.0 0.0 copy-done.5
  120.0 6.5 %project.1 = bf16[8,256,256]{2,1,0:T(8,128)(2,1)} custom-call(bf16[128,1024]{1,0:T(8,128)(2,1)} %copy-done, bf16[128,1024]{1,0:T(8,128)(2,1)} %copy-done.5, bf16[16,1024,128]{2,1,0:T(8,128)(2,1)} %bitcast.8), custom_call_target="tpu_custom_call" | custom-call | flops 1000000000 | bytes 10000000 | tf_op jit(solution)/shard_map/project/pallas_call | solution.py:193
  126.5 27.0 %all_to_all.11.terms_ref = bf16[8,256,256]{2,1,0:T(8,128)(2,1)S(1)} all-to-all(bf16[8,256,256]{2,1,0:T(8,128)(2,1)} %project.1), channel_id=1, replica_groups=mesh['groups'=2,'z'=16,'core'=2,'tp'=8] {'tp'}, dimensions={0} | all-to-all | bytes 2097152 | tf_op jit(solution)/shard_map/all_to_all | solution.py:206
  153.5 0.1 total.1
  153.7 11.6 %collective-permute-start.3 = (bf16[128,256]{1,0:T(8,128)(2,1)S(1)}, bf16[128,256]{1,0:T(8,128)(2,1)S(1)}, u32[]{:S(2)}, u32[]{:S(2)}) collective-permute-start(bf16[128,256]{1,0:T(8,128)(2,1)S(1)} %get-tuple-element.16), channel_id=1, source_target_pairs={{0,8},{8,0},{1,9},{9,1},{2,10},{10,2},{3,11},{11,3},{4,12},{12,4},... | collective-permute-start | bytes 196616 | tf_op jit(solution)/shard_map/ppermute | solution.py:216
  165.3 0.9 collective-permute-done.3.given_ref
  166.2 0.7 weave.1
  (2 shorter events, 0.0 us)
Async XLA Ops:
  6.5 113.5 %all-gather.4.cloned.1.call-start = ((), (), s32[]{:S(2)}) async-start(), calls=%async_computation.2 | async-start | bytes 4456448 | tf_op jit(solution)/shard_map/all_gather | solution.py:147
  7.7 1.0 copy-start.1
  8.6 0.8 copy-start.2
  9.4 0.8 copy-start.3
  10.1 0.7 copy-start.4
  84.2 29.8 %collective-permute-start = (bf16[16,248,128]{2,1,0:T(8,128)(2,1)S(1)}, bf16[16,248,128]{2,1,0:T(8,128)(2,1)S(1)}, u32[]{:S(2)}, u32[]{:S(2)}) collective-permute-start(bf16[16,248,128]{2,1,0:T(8,128)(2,1)S(1)} %bitcast.5), channel_id=1, source_target_pairs={{0,8},{8,0},{1,9},{9,1},{2,10},{10,2},{3,11},{11,3},{4,12},{12,4},... | collective-permute-start | bytes 3047432 | tf_op jit(solution)/shard_map/ppermute | solution.py:171
  109.9 4.1 %collective-permute-start.1 = (bf16[16,8,128]{2,1,0:T(8,128)(2,1)S(1)}, bf16[16,8,128]{2,1,0:T(8,128)(2,1)S(1)}, u32[]{:S(2)}, u32[]{:S(2)}) collective-permute-start(bf16[16,8,128]{2,1,0:T(8,128)(2,1)S(1)} %all_to_all.10.resta_ref), channel_id=1, source_target_pairs={{0,8},{8,0},{1,9},{9,1},{2,10},{10,2},{3,11},{11,3},{4,12},{12,4},... | collective-permute-start | bytes 98312 | tf_op jit(solution)/shard_map/ppermute | solution.py:173
  115.2 4.8 %copy-start = (bf16[128,1024]{1,0:T(8,128)(2,1)}, bf16[128,1024]{1,0:T(8,128)(2,1)S(1)}, u32[]{:S(2)}) copy-start(bf16[128,1024]{1,0:T(8,128)(2,1)S(1)} %attend.1.own_ref) | copy-start | bytes 786436
  115.2 3.5 %collective-permute-start.2 = (bf16[128,1024]{1,0:T(8,128)(2,1)S(1)}, bf16[128,1024]{1,0:T(8,128)(2,1)S(1)}, u32[]{:S(2)}, u32[]{:S(2)}) collective-permute-start(bf16[128,1024]{1,0:T(8,128)(2,1)S(1)} %attend.1.own_ref), channel_id=1, source_target_pairs={{0,8},{8,0},{1,9},{9,1},{2,10},{10,2},{3,11},{11,3},{4,12},{12,4},... | collective-permute-start | bytes 786440 | tf_op jit(solution)/shard_map/ppermute | solution.py:190
  118.6 1.4 copy-start.5
  153.7 12.5 %collective-permute-start.3 = (bf16[128,256]{1,0:T(8,128)(2,1)S(1)}, bf16[128,256]{1,0:T(8,128)(2,1)S(1)}, u32[]{:S(2)}, u32[]{:S(2)}) collective-permute-start(bf16[128,256]{1,0:T(8,128)(2,1)S(1)} %get-tuple-element.16), channel_id=1, source_target_pairs={{0,8},{8,0},{1,9},{9,1},{2,10},{10,2},{3,11},{11,3},{4,12},{12,4},... | collective-permute-start | bytes 196616 | tf_op jit(solution)/shard_map/ppermute | solution.py:216
Sparse Core Ops, SparseCore 0:
  9.4 110.5 all-gather.3

commit v9 on v8

--- a/solution.py
+++ b/solution.py
@@ -113,12 +113,16 @@
     for copy in copies:
         copy.start()
     both = jnp.concatenate([own_ref[...], other_ref[...]], 0)
-    for i, copy in enumerate(copies):
-        copy.wait()
-        weights = jnp.concatenate([w_ref[i * share + j] for j in range(share)], 1)
-        out_ref[i] = jnp.dot(both, weights, preferred_element_type=jnp.float32).astype(
-            jnp.bfloat16
-        )
+    width = out_ref.shape[2]
+    group = math.gcd(parts, 2)
+    for g in range(0, parts, group):
+        for copy in copies[g : g + group]:
+            copy.wait()
+        blocks = range(g * share, (g + group) * share)
+        weights = jnp.concatenate([w_ref[j] for j in blocks], 1)
+        terms = jnp.dot(both, weights, preferred_element_type=jnp.float32).astype(jnp.bfloat16)
+        for i in range(group):
+            out_ref[g + i] = terms[:, i * width : (i + 1) * width]
 
 
 def total(terms_ref, kept_ref, sent_ref):

time: 174 us -> 173 us (level)
  no operation moved by 1% of the time
where the time goes in v9:
time: 173 us; the launch traced here: 172 us
  blocking collectives  116 us (67%)
  starting transfers between devices  26.9 us (16%)
  between operations  13.5 us (8%)
  Pallas kernels  7.28 us (4%)
  waiting for transfers between devices  5.01 us (3%)
  local copies, waits for them, and re-layouts  3.18 us (2%)
    all_gather x1, blocking collectives, on_device(): most_a = lax.all_gather(here, 'z', axis=0, tiled=False)  73.1 us
    all_to_all x1, blocking collectives, on_device(): lax.all_to_all(terms, 'tp', split_axis=0, concat_axis=0, tiled=True)  27 us
    all_to_all x1, blocking collectives, on_device(): lax.all_to_all(rest_here, 'z', split_axis=0, concat_axis=0, tiled=True)  15.9 us
    ppermute x1, starting transfers between devices, on_device(): given = lax.ppermute(sent, 'core', swap)  11.6 us
    ppermute x1, starting transfers between devices, on_device(): most_b = lax.ppermute(most_a, 'core', swap)  9.74 us
    pallas_call x1, Pallas kernels, on_device(): pl.pallas_call(functools.partial(project, share), out_shape=jax.ShapeDtyp...  5.05 us
  transfers between devices with their start and end apart: 5, of which 4 were waited for; matrix products, arithmetic and copies ran while one was open for 0% of the time, Pallas kernels for 1%

profile of v9, /device:TPU:65, one launch (start us, length us, event | category | flops | bytes accessed | tf_op | source)
XLA Modules:
  0.0 172.3 jit_solution(14695567605776186584)
XLA Ops:
  6.5 0.0 all-gather.4.cloned.1.call-start
  6.6 0.7 all-gather.4.cloned.1.call-update
  7.3 0.3 fusion
  7.7 0.0 copy-start.1
  7.7 0.9 copy-done.1
  8.6 0.0 copy-start.2
  8.6 0.8 copy-done.2
  9.4 0.0 copy-start.3
  9.4 0.8 copy-done.3
  10.1 0.0 copy-start.4
  10.1 0.7 copy-done.4
  10.8 0.2 prepare.1
  11.1 73.1 %all-gather = bf16[3968,128]{1,0:T(8,128)(2,1)S(1)} all-gather(bf16[248,128]{1,0:T(8,128)(2,1)S(1)} %get-tuple-element.13), channel_id=2, replica_groups=mesh['groups'=2,'z'=16,'core'=2,'tp'=8] {'z'}, dimensions={0}, use_global_device_ids=true | all-gather | bytes 1079296 | tf_op jit(solution)/shard_map/all_gather | solution.py:174
  84.2 9.7 %collective-permute-start = (bf16[16,248,128]{2,1,0:T(8,128)(2,1)S(1)}, bf16[16,248,128]{2,1,0:T(8,128)(2,1)S(1)}, u32[]{:S(2)}, u32[]{:S(2)}) collective-permute-start(bf16[16,248,128]{2,1,0:T(8,128)(2,1)S(1)} %bitcast.5), channel_id=1, source_target_pairs={{0,8},{8,0},{1,9},{9,1},{2,10},{10,2},{3,11},{11,3},{4,12},{12,4},... | collective-permute-start | bytes 3047432 | tf_op jit(solution)/shard_map/ppermute | solution.py:175
  93.9 15.9 %all_to_all.10.resta_ref = bf16[16,8,128]{2,1,0:T(8,128)(2,1)S(1)} all-to-all(bf16[16,8,128]{2,1,0:T(8,128)(2,1)S(1)} %get-tuple-element.14), channel_id=1, replica_groups=mesh['groups'=2,'z'=16,'core'=2,'tp'=8] {'z'}, dimensions={0} | all-to-all | bytes 65536 | tf_op jit(solution)/shard_map/all_to_all | solution.py:176
  109.9 3.2 %collective-permute-start.1 = (bf16[16,8,128]{2,1,0:T(8,128)(2,1)S(1)}, bf16[16,8,128]{2,1,0:T(8,128)(2,1)S(1)}, u32[]{:S(2)}, u32[]{:S(2)}) collective-permute-start(bf16[16,8,128]{2,1,0:T(8,128)(2,1)S(1)} %all_to_all.10.resta_ref), channel_id=1, source_target_pairs={{0,8},{8,0},{1,9},{9,1},{2,10},{10,2},{3,11},{11,3},{4,12},{12,4},... | collective-permute-start | bytes 98312 | tf_op jit(solution)/shard_map/ppermute | solution.py:177
  113.1 0.8 collective-permute-done.1.restb_ref
  114.0 0.0 collective-permute-done.b_ref
  114.0 1.2 attend.1.own_ref
  115.2 0.0 copy-start
  115.2 2.3 %collective-permute-start.2 = (bf16[128,1024]{1,0:T(8,128)(2,1)S(1)}, bf16[128,1024]{1,0:T(8,128)(2,1)S(1)}, u32[]{:S(2)}, u32[]{:S(2)}) collective-permute-start(bf16[128,1024]{1,0:T(8,128)(2,1)S(1)} %attend.1.own_ref), channel_id=1, source_target_pairs={{0,8},{8,0},{1,9},{9,1},{2,10},{10,2},{3,11},{11,3},{4,12},{12,4},... | collective-permute-start | bytes 786440 | tf_op jit(solution)/shard_map/ppermute | solution.py:194
  117.5 1.2 collective-permute-done.2.other_ref
  118.6 0.0 copy-start.5
  118.6 1.4 all-gather.4.cloned.1.call-done
  120.0 0.0 copy-done
  120.0 0.0 copy-done.5
  120.0 5.0 %project.1 = bf16[8,256,256]{2,1,0:T(8,128)(2,1)} custom-call(bf16[128,1024]{1,0:T(8,128)(2,1)} %copy-done, bf16[128,1024]{1,0:T(8,128)(2,1)} %copy-done.5, bf16[16,1024,128]{2,1,0:T(8,128)(2,1)} %bitcast.8), custom_call_target="tpu_custom_call" | custom-call | flops 1000000000 | bytes 10000000 | tf_op jit(solution)/shard_map/project/pallas_call | solution.py:197
  125.1 27.0 %all_to_all.11.terms_ref = bf16[8,256,256]{2,1,0:T(8,128)(2,1)S(1)} all-to-all(bf16[8,256,256]{2,1,0:T(8,128)(2,1)} %project.1), channel_id=1, replica_groups=mesh['groups'=2,'z'=16,'core'=2,'tp'=8] {'tp'}, dimensions={0} | all-to-all | bytes 2097152 | tf_op jit(solution)/shard_map/all_to_all | solution.py:210
  152.1 0.1 total.1
  152.2 11.6 %collective-permute-start.3 = (bf16[128,256]{1,0:T(8,128)(2,1)S(1)}, bf16[128,256]{1,0:T(8,128)(2,1)S(1)}, u32[]{:S(2)}, u32[]{:S(2)}) collective-permute-start(bf16[128,256]{1,0:T(8,128)(2,1)S(1)} %get-tuple-element.16), channel_id=1, source_target_pairs={{0,8},{8,0},{1,9},{9,1},{2,10},{10,2},{3,11},{11,3},{4,12},{12,4},... | collective-permute-start | bytes 196616 | tf_op jit(solution)/shard_map/ppermute | solution.py:220
  163.9 0.9 collective-permute-done.3.given_ref
  164.8 0.7 weave.1
  (2 shorter events, 0.0 us)
Async XLA Ops:
  6.5 113.5 %all-gather.4.cloned.1.call-start = ((), (), s32[]{:S(2)}) async-start(), calls=%async_computation.2 | async-start | bytes 4456448 | tf_op jit(solution)/shard_map/all_gather | solution.py:151
  7.7 1.0 copy-start.1
  8.6 0.8 copy-start.2
  9.4 0.8 copy-start.3
  10.1 0.7 copy-start.4
  84.2 29.8 %collective-permute-start = (bf16[16,248,128]{2,1,0:T(8,128)(2,1)S(1)}, bf16[16,248,128]{2,1,0:T(8,128)(2,1)S(1)}, u32[]{:S(2)}, u32[]{:S(2)}) collective-permute-start(bf16[16,248,128]{2,1,0:T(8,128)(2,1)S(1)} %bitcast.5), channel_id=1, source_target_pairs={{0,8},{8,0},{1,9},{9,1},{2,10},{10,2},{3,11},{11,3},{4,12},{12,4},... | collective-permute-start | bytes 3047432 | tf_op jit(solution)/shard_map/ppermute | solution.py:175
  109.9 4.1 %collective-permute-start.1 = (bf16[16,8,128]{2,1,0:T(8,128)(2,1)S(1)}, bf16[16,8,128]{2,1,0:T(8,128)(2,1)S(1)}, u32[]{:S(2)}, u32[]{:S(2)}) collective-permute-start(bf16[16,8,128]{2,1,0:T(8,128)(2,1)S(1)} %all_to_all.10.resta_ref), channel_id=1, source_target_pairs={{0,8},{8,0},{1,9},{9,1},{2,10},{10,2},{3,11},{11,3},{4,12},{12,4},... | collective-permute-start | bytes 98312 | tf_op jit(solution)/shard_map/ppermute | solution.py:177
  115.2 4.8 %copy-start = (bf16[128,1024]{1,0:T(8,128)(2,1)}, bf16[128,1024]{1,0:T(8,128)(2,1)S(1)}, u32[]{:S(2)}) copy-start(bf16[128,1024]{1,0:T(8,128)(2,1)S(1)} %attend.1.own_ref) | copy-start | bytes 786436
  115.2 3.5 %collective-permute-start.2 = (bf16[128,1024]{1,0:T(8,128)(2,1)S(1)}, bf16[128,1024]{1,0:T(8,128)(2,1)S(1)}, u32[]{:S(2)}, u32[]{:S(2)}) collective-permute-start(bf16[128,1024]{1,0:T(8,128)(2,1)S(1)} %attend.1.own_ref), channel_id=1, source_target_pairs={{0,8},{8,0},{1,9},{9,1},{2,10},{10,2},{3,11},{11,3},{4,12},{12,4},... | collective-permute-start | bytes 786440 | tf_op jit(solution)/shard_map/ppermute | solution.py:194
  118.6 1.4 copy-start.5
  152.2 12.5 %collective-permute-start.3 = (bf16[128,256]{1,0:T(8,128)(2,1)S(1)}, bf16[128,256]{1,0:T(8,128)(2,1)S(1)}, u32[]{:S(2)}, u32[]{:S(2)}) collective-permute-start(bf16[128,256]{1,0:T(8,128)(2,1)S(1)} %get-tuple-element.16), channel_id=1, source_target_pairs={{0,8},{8,0},{1,9},{9,1},{2,10},{10,2},{3,11},{11,3},{4,12},{12,4},... | collective-permute-start | bytes 196616 | tf_op jit(solution)/shard_map/ppermute | solution.py:220
Sparse Core Ops, SparseCore 0:
  9.4 110.5 all-gather.3

commit v10 on v9

--- a/solution.py
+++ b/solution.py
@@ -114,7 +114,7 @@
         copy.start()
     both = jnp.concatenate([own_ref[...], other_ref[...]], 0)
     width = out_ref.shape[2]
-    group = math.gcd(parts, 2)
+    group = math.gcd(parts, 4)
     for g in range(0, parts, group):
         for copy in copies[g : g + group]:
             copy.wait()

time: 173 us -> 173 us (level)
  no operation moved by 1% of the time
where the time goes in v10:
time: 173 us; the launch traced here: 172 us
  blocking collectives  116 us (67%)
  starting transfers between devices  26.9 us (16%)
  between operations  13.5 us (8%)
  Pallas kernels  7.26 us (4%)
  waiting for transfers between devices  5.01 us (3%)
  local copies, waits for them, and re-layouts  3.18 us (2%)
    all_gather x1, blocking collectives, on_device(): most_a = lax.all_gather(here, 'z', axis=0, tiled=False)  73.1 us
    all_to_all x1, blocking collectives, on_device(): lax.all_to_all(terms, 'tp', split_axis=0, concat_axis=0, tiled=True)  27 us
    all_to_all x1, blocking collectives, on_device(): lax.all_to_all(rest_here, 'z', split_axis=0, concat_axis=0, tiled=True)  15.9 us
    ppermute x1, starting transfers between devices, on_device(): given = lax.ppermute(sent, 'core', swap)  11.6 us
    ppermute x1, starting transfers between devices, on_device(): most_b = lax.ppermute(most_a, 'core', swap)  9.74 us
    pallas_call x1, Pallas kernels, on_device(): pl.pallas_call(functools.partial(project, share), out_shape=jax.ShapeDtyp...  5.03 us
  transfers between devices with their start and end apart: 5, of which 4 were waited for; matrix products, arithmetic and copies ran while one was open for 0% of the time, Pallas kernels for 1%

profile of v10, /device:TPU:65, one launch (start us, length us, event | category | flops | bytes accessed | tf_op | source)
XLA Modules:
  0.0 172.3 jit_solution(15189562184356163427)
XLA Ops:
  6.5 0.0 all-gather.4.cloned.1.call-start
  6.6 0.7 all-gather.4.cloned.1.call-update
  7.3 0.3 fusion
  7.7 0.0 copy-start.1
  7.7 0.9 copy-done.1
  8.6 0.0 copy-start.2
  8.6 0.8 copy-done.2
  9.4 0.0 copy-start.3
  9.4 0.8 copy-done.3
  10.1 0.0 copy-start.4
  10.1 0.7 copy-done.4
  10.8 0.2 prepare.1
  11.1 73.1 %all-gather = bf16[3968,128]{1,0:T(8,128)(2,1)S(1)} all-gather(bf16[248,128]{1,0:T(8,128)(2,1)S(1)} %get-tuple-element.13), channel_id=2, replica_groups=mesh['groups'=2,'z'=16,'core'=2,'tp'=8] {'z'}, dimensions={0}, use_global_device_ids=true | all-gather | bytes 1079296 | tf_op jit(solution)/shard_map/all_gather | solution.py:174
  84.2 9.7 %collective-permute-start = (bf16[16,248,128]{2,1,0:T(8,128)(2,1)S(1)}, bf16[16,248,128]{2,1,0:T(8,128)(2,1)S(1)}, u32[]{:S(2)}, u32[]{:S(2)}) collective-permute-start(bf16[16,248,128]{2,1,0:T(8,128)(2,1)S(1)} %bitcast.5), channel_id=1, source_target_pairs={{0,8},{8,0},{1,9},{9,1},{2,10},{10,2},{3,11},{11,3},{4,12},{12,4},... | collective-permute-start | bytes 3047432 | tf_op jit(solution)/shard_map/ppermute | solution.py:175
  93.9 15.9 %all_to_all.10.resta_ref = bf16[16,8,128]{2,1,0:T(8,128)(2,1)S(1)} all-to-all(bf16[16,8,128]{2,1,0:T(8,128)(2,1)S(1)} %get-tuple-element.14), channel_id=1, replica_groups=mesh['groups'=2,'z'=16,'core'=2,'tp'=8] {'z'}, dimensions={0} | all-to-all | bytes 65536 | tf_op jit(solution)/shard_map/all_to_all | solution.py:176
  109.9 3.2 %collective-permute-start.1 = (bf16[16,8,128]{2,1,0:T(8,128)(2,1)S(1)}, bf16[16,8,128]{2,1,0:T(8,128)(2,1)S(1)}, u32[]{:S(2)}, u32[]{:S(2)}) collective-permute-start(bf16[16,8,128]{2,1,0:T(8,128)(2,1)S(1)} %all_to_all.10.resta_ref), channel_id=1, source_target_pairs={{0,8},{8,0},{1,9},{9,1},{2,10},{10,2},{3,11},{11,3},{4,12},{12,4},... | collective-permute-start | bytes 98312 | tf_op jit(solution)/shard_map/ppermute | solution.py:177
  113.1 0.8 collective-permute-done.1.restb_ref
  114.0 0.0 collective-permute-done.b_ref
  114.0 1.2 attend.1.own_ref
  115.2 0.0 copy-start
  115.2 2.3 %collective-permute-start.2 = (bf16[128,1024]{1,0:T(8,128)(2,1)S(1)}, bf16[128,1024]{1,0:T(8,128)(2,1)S(1)}, u32[]{:S(2)}, u32[]{:S(2)}) collective-permute-start(bf16[128,1024]{1,0:T(8,128)(2,1)S(1)} %attend.1.own_ref), channel_id=1, source_target_pairs={{0,8},{8,0},{1,9},{9,1},{2,10},{10,2},{3,11},{11,3},{4,12},{12,4},... | collective-permute-start | bytes 786440 | tf_op jit(solution)/shard_map/ppermute | solution.py:194
  117.5 1.2 collective-permute-done.2.other_ref
  118.6 0.0 copy-start.5
  118.6 1.4 all-gather.4.cloned.1.call-done
  120.0 0.0 copy-done
  120.0 0.0 copy-done.5
  120.0 5.0 %project.1 = bf16[8,256,256]{2,1,0:T(8,128)(2,1)} custom-call(bf16[128,1024]{1,0:T(8,128)(2,1)} %copy-done, bf16[128,1024]{1,0:T(8,128)(2,1)} %copy-done.5, bf16[16,1024,128]{2,1,0:T(8,128)(2,1)} %bitcast.8), custom_call_target="tpu_custom_call" | custom-call | flops 1000000000 | bytes 10000000 | tf_op jit(solution)/shard_map/project/pallas_call | solution.py:197
  125.0 27.0 %all_to_all.11.terms_ref = bf16[8,256,256]{2,1,0:T(8,128)(2,1)S(1)} all-to-all(bf16[8,256,256]{2,1,0:T(8,128)(2,1)} %project.1), channel_id=1, replica_groups=mesh['groups'=2,'z'=16,'core'=2,'tp'=8] {'tp'}, dimensions={0} | all-to-all | bytes 2097152 | tf_op jit(solution)/shard_map/all_to_all | solution.py:210
  152.1 0.1 total.1
  152.2 11.6 %collective-permute-start.3 = (bf16[128,256]{1,0:T(8,128)(2,1)S(1)}, bf16[128,256]{1,0:T(8,128)(2,1)S(1)}, u32[]{:S(2)}, u32[]{:S(2)}) collective-permute-start(bf16[128,256]{1,0:T(8,128)(2,1)S(1)} %get-tuple-element.16), channel_id=1, source_target_pairs={{0,8},{8,0},{1,9},{9,1},{2,10},{10,2},{3,11},{11,3},{4,12},{12,4},... | collective-permute-start | bytes 196616 | tf_op jit(solution)/shard_map/ppermute | solution.py:220
  163.9 0.9 collective-permute-done.3.given_ref
  164.7 0.7 weave.1
  (2 shorter events, 0.0 us)
Async XLA Ops:
  6.5 113.5 %all-gather.4.cloned.1.call-start = ((), (), s32[]{:S(2)}) async-start(), calls=%async_computation.2 | async-start | bytes 4456448 | tf_op jit(solution)/shard_map/all_gather | solution.py:151
  7.7 1.0 copy-start.1
  8.6 0.8 copy-start.2
  9.4 0.8 copy-start.3
  10.1 0.7 copy-start.4
  84.2 29.8 %collective-permute-start = (bf16[16,248,128]{2,1,0:T(8,128)(2,1)S(1)}, bf16[16,248,128]{2,1,0:T(8,128)(2,1)S(1)}, u32[]{:S(2)}, u32[]{:S(2)}) collective-permute-start(bf16[16,248,128]{2,1,0:T(8,128)(2,1)S(1)} %bitcast.5), channel_id=1, source_target_pairs={{0,8},{8,0},{1,9},{9,1},{2,10},{10,2},{3,11},{11,3},{4,12},{12,4},... | collective-permute-start | bytes 3047432 | tf_op jit(solution)/shard_map/ppermute | solution.py:175
  109.9 4.1 %collective-permute-start.1 = (bf16[16,8,128]{2,1,0:T(8,128)(2,1)S(1)}, bf16[16,8,128]{2,1,0:T(8,128)(2,1)S(1)}, u32[]{:S(2)}, u32[]{:S(2)}) collective-permute-start(bf16[16,8,128]{2,1,0:T(8,128)(2,1)S(1)} %all_to_all.10.resta_ref), channel_id=1, source_target_pairs={{0,8},{8,0},{1,9},{9,1},{2,10},{10,2},{3,11},{11,3},{4,12},{12,4},... | collective-permute-start | bytes 98312 | tf_op jit(solution)/shard_map/ppermute | solution.py:177
  115.2 4.8 %copy-start = (bf16[128,1024]{1,0:T(8,128)(2,1)}, bf16[128,1024]{1,0:T(8,128)(2,1)S(1)}, u32[]{:S(2)}) copy-start(bf16[128,1024]{1,0:T(8,128)(2,1)S(1)} %attend.1.own_ref) | copy-start | bytes 786436
  115.2 3.5 %collective-permute-start.2 = (bf16[128,1024]{1,0:T(8,128)(2,1)S(1)}, bf16[128,1024]{1,0:T(8,128)(2,1)S(1)}, u32[]{:S(2)}, u32[]{:S(2)}) collective-permute-start(bf16[128,1024]{1,0:T(8,128)(2,1)S(1)} %attend.1.own_ref), channel_id=1, source_target_pairs={{0,8},{8,0},{1,9},{9,1},{2,10},{10,2},{3,11},{11,3},{4,12},{12,4},... | collective-permute-start | bytes 786440 | tf_op jit(solution)/shard_map/ppermute | solution.py:194
  118.6 1.4 copy-start.5
  152.2 12.5 %collective-permute-start.3 = (bf16[128,256]{1,0:T(8,128)(2,1)S(1)}, bf16[128,256]{1,0:T(8,128)(2,1)S(1)}, u32[]{:S(2)}, u32[]{:S(2)}) collective-permute-start(bf16[128,256]{1,0:T(8,128)(2,1)S(1)} %get-tuple-element.16), channel_id=1, source_target_pairs={{0,8},{8,0},{1,9},{9,1},{2,10},{10,2},{3,11},{11,3},{4,12},{12,4},... | collective-permute-start | bytes 196616 | tf_op jit(solution)/shard_map/ppermute | solution.py:220
Sparse Core Ops, SparseCore 0:
  9.4 110.5 all-gather.3
